TPU v7x, 32 devices: a whole 2x2x4 slice. The times are simulated.
32 devices in a mesh: heads: 4 (over y, x), seq: 8 (over z, core).
Axes of the slice: x: 2, y: 2, z: 4, core: 2. Of those that a mesh axis runs over, the one named last changes fastest.
Arguments:
- query: bfloat16 [24, 128, 576], P(None, 'heads'), may hold values from -1024 to 1024
- cache: bfloat16 [4096, 576], P('seq'), may hold values from -8 to 8
- segments: int32 [4096], P('seq'), may hold values from 0 to 3, as said below
- groups: int32 [24], replicated, may hold values from 0 to 3
- value_up: bfloat16 [128, 512, 128], P('heads'), may hold values from -3 to 3
- out_proj: bfloat16 [16384, 7168], P('heads', 'seq'), may hold values from -0.046875 to 0.046875
- targets: float32 [24, 7168], P(None, 'seq'), may hold values from -20 to 20
Outputs:
- projected: float32 [24, 7168], P(None, 'seq')
- loss: float32 [], replicated
- query_grad: float32 [24, 128, 576], P(None, 'heads')
- cache_grad: float32 [4096, 576], P('seq', 'heads')
Inputs may be any that keep to these rules, and one draw needn't show every extreme that they name: `segments`: constant over each aligned tile of 128 cached tokens; every group number appears in some tile.
All inputs are finite; a program needn't handle non-finite values.
Results may differ from a plain program's by a relative error of at most 0.015.
Values may be sent and summed in bfloat16 or wider, within the bound.
No kernel may reach another device: no remote copies, remote signals or barrier semaphores. Data moves between devices by JAX's collectives and lax.ppermute only.
A program may use at most 64 MiB of HBM per device.

v0:
```python
import jax
import jax.numpy as jnp
from jax import lax
from jax.sharding import PartitionSpec as P

scale_factor = 0.07216878364870322
floor_value = -1e30


def on_device(query, cache, segments, groups, value_up, out_proj, targets):
    query_len, head_count, width = query.shape
    latent = value_up.shape[1]
    vwidth = value_up.shape[2]
    row_count = query_len * head_count
    cache_len = cache.shape[0]
    query_rows = query.reshape(row_count, width)
    values = cache[:, :latent]
    allowed = groups[:, None] == segments[None, :]
    allowed_rows = jnp.broadcast_to(
        allowed[:, None, :], (query_len, head_count, cache_len)
    ).reshape(row_count, cache_len)
    scores = (
        jnp.einsum("rc,tc->rt", query_rows, cache, preferred_element_type=jnp.float32)
        * scale_factor
    )
    masked = jnp.where(allowed_rows, scores, floor_value)
    local_top = jnp.max(masked, axis=1)
    maximum = lax.pmax(local_top, "seq")
    weights = jnp.where(allowed_rows, jnp.exp(masked - maximum[:, None]), 0.0)
    totals = lax.psum(jnp.sum(weights, axis=1), "seq")
    partial_latent = jnp.dot(
        weights.astype(jnp.bfloat16), values, preferred_element_type=jnp.float32
    )
    portion = lax.psum_scatter(partial_latent, "seq", scatter_dimension=0, tiled=True)
    share_rows = portion.shape[0]
    start = lax.axis_index("seq") * share_rows
    share_totals = lax.dynamic_slice_in_dim(totals, start, share_rows)
    share_latent = (portion / share_totals[:, None]).astype(jnp.bfloat16)
    head_ids = (start + jnp.arange(share_rows, dtype=jnp.int32)) % head_count
    row_weights = jnp.take(value_up, head_ids, axis=0)
    share_value = jnp.einsum(
        "rc,rcv->rv", share_latent, row_weights, preferred_element_type=jnp.float32
    ).astype(jnp.bfloat16)
    value_out = lax.all_gather(share_value, "seq", axis=0, tiled=True).reshape(
        query_len, head_count, vwidth
    )
    flattened = value_out.reshape(query_len, head_count * vwidth)
    partial_proj = jnp.dot(flattened, out_proj, preferred_element_type=jnp.float32)
    projected = lax.psum(partial_proj, "heads")
    residual = projected - targets
    square_part = jnp.sum(residual * residual)
    model_width = targets.shape[1] * lax.axis_size("seq")
    d_projected = residual.astype(jnp.bfloat16)
    value_partial = jnp.einsum(
        "qd,rd->qr", d_projected, out_proj, preferred_element_type=jnp.float32
    )
    d_value = lax.psum(value_partial, "seq").reshape(query_len, head_count, vwidth)
    d_latent = (
        jnp.einsum(
            "qhv,hcv->qhc",
            d_value.astype(jnp.bfloat16),
            value_up,
            preferred_element_type=jnp.float32,
        )
        .astype(jnp.bfloat16)
        .reshape(row_count, latent)
    )
    row_dot = jnp.sum(d_value * value_out.astype(jnp.float32), axis=2).reshape(row_count)
    probs = weights / totals[:, None]
    d_probs = jnp.einsum("rc,tc->rt", d_latent, values, preferred_element_type=jnp.float32)
    d_scores = (scale_factor * probs * (d_probs - row_dot[:, None])).astype(jnp.bfloat16)
    query_part = jnp.dot(d_scores, cache, preferred_element_type=jnp.float32)
    square_total = lax.psum(square_part, "seq")
    query_sum = lax.psum(query_part, "seq")
    loss = square_total / (query_len * model_width)
    query_grad = query_sum.reshape(query_len, head_count, width)
    key_part = jnp.einsum("rt,rc->tc", d_scores, query_rows, preferred_element_type=jnp.float32)
    value_part = jnp.einsum(
        "rt,rc->tc", probs.astype(jnp.bfloat16), d_latent, preferred_element_type=jnp.float32
    )
    cache_part = key_part + jnp.concatenate(
        [value_part, jnp.zeros((cache_len, width - latent), jnp.float32)], axis=1
    )
    cache_grad = lax.psum_scatter(
        cache_part.astype(jnp.bfloat16), "heads", scatter_dimension=1, tiled=True
    ).astype(jnp.float32)
    return (projected, loss, query_grad, cache_grad)


def solution(mesh):
    in_specs = (
        P(None, "heads", None),
        P("seq", None),
        P("seq"),
        P(),
        P("heads", None, None),
        P("heads", "seq"),
        P(None, "seq"),
    )
    out_specs = (P(None, "seq"), P(), P(None, "heads", None), P("seq", "heads"))
    return jax.shard_map(
        on_device, mesh=mesh, in_specs=in_specs, out_specs=out_specs, check_vma=False
    )
```

profile of v0, /device:TPU:0, one launch (start us, length us, event | category | flops | bytes accessed | tf_op | source)
XLA Modules:
  0.0 309.5 jit_solution(6097966343069492329)
XLA Ops:
  7.2 0.0 copy-start
  7.2 0.0 reduce-scatter.3.cloned.1.call-start
  7.2 0.8 broadcast_compare_fusion
  8.1 0.1 broadcast_in_dim.29
  8.2 0.5 copy.29
  8.7 0.0 copy-done
  8.7 0.0 copy-start.2
  8.7 2.0 fusion.25
  10.7 18.1 %pmax.7 = f32[768]{0:T(1024)S(1)} all-reduce(f32[768]{0:T(1024)S(1)} %get-tuple-element.4), channel_id=1, replica_groups=mesh['heads'=4,'seq'=8] {'seq'}, use_global_device_ids=true, to_apply=%region_1.2 | all-reduce | flops 768 | bytes 6144 | tf_op jit(solution)/shard_map/pmax | solution.py:28
  28.8 0.0 copy-start.5
  28.8 0.0 copy-done.2
  28.8 1.8 fusion.8
  30.6 0.0 reduce-scatter.3.cloned.1.call-update
  30.6 0.0 all-reduce.5.cloned.1.call-start
  30.7 0.0 copy-done.5
  30.7 0.4 fusion.15
  31.1 13.7 %psum.35 = f32[768]{0:T(1024)S(1)} all-reduce(f32[768]{0:T(1024)S(1)} %fusion.15), channel_id=1, replica_groups=mesh['heads'=4,'seq'=8] {'seq'}, use_global_device_ids=true, to_apply=%region_4.5 | all-reduce | flops 768 | bytes 6144 | tf_op jit(solution)/shard_map/psum | solution.py:30
  44.8 0.0 copy-start.7
  44.8 0.1 dynamic_slice.3
  44.9 0.5 copy-done.7
  45.4 8.8 %gather_fusion = bf16[96,512,128]{2,1,0:T(8,128)(2,1)} fusion(bf16[32,512,128]{2,1,0:T(8,128)(2,1)} %param.11, s32[1024]{0:T(1024)S(1)} %pad_clamp_fusion), kind=kCustom, calls=%fused_computation | custom fusion | bytes 25166208 | tf_op jit(solution)/shard_map/jit(_take)/gather | solution.py:40
  54.2 9.3 %reduce-scatter.3.cloned.1.call-done = f32[96,512]{1,0:T(8,128)} async-done(((f32[768,512]{1,0:T(8,128)}), f32[96,512]{1,0:T(8,128)}) %reduce-scatter.3.cloned.1.call-update) | async-done | bytes 196624 | tf_op jit(solution)/shard_map/reduce_scatter | solution.py:34
  63.5 1.0 fusion.16
  64.5 5.7 %fusion = f32[96,1,128]{2,1,0:T(1,128)S(1)} fusion(bf16[96,512,128]{2,1,0:T(8,128)(2,1)} %gather_fusion, pred[96]{0:T(512)(128)(4,1)S(1)} %compare_and_fusion, bf16[96,512,1]{1,0,2:T(8,128)(2,1)S(1)} %fusion.16), kind=kOutput, calls=%fused_computation.1 | convolution fusion | flops 18874368 | bytes 12730464 | tf_op jit(solution)/shard_map/rc,rcv->rv/dot_general | solution.py:41
  70.3 15.2 %all_gather.3 = bf16[768,128]{1,0:T(8,128)(2,1)} all-gather(bf16[96,128]{1,0:T(8,128)(2,1)S(1)} %convert_element_type.41), channel_id=1, replica_groups=mesh['heads'=4,'seq'=8] {'seq'}, dimensions={0}, use_global_device_ids=true | all-gather | bytes 221184 | tf_op jit(solution)/shard_map/all_gather | solution.py:44
  85.4 1.7 reshape_reshape.3
  87.1 4.9 %fusion.26 = f32[24,896]{1,0:T(8,128)} fusion(bf16[24,4096]{1,0:T(8,128)(2,1)} %reshape_reshape.3, bf16[4096,896]{1,0:T(8,128)(2,1)} %param.12), kind=kOutput, calls=%fused_computation.49 | convolution fusion | flops 176160768 | bytes 7622656 | tf_op jit(solution)/shard_map/dot_general | solution.py:48
  92.0 0.0 all-reduce.5.cloned.1.call-update
  92.0 0.0 all-reduce.7.cloned.1.call-start
  92.1 39.5 %all-reduce.5.cloned.1.call-done = f32[24,896]{1,0:T(8,128)} async-done(((f32[24,896]{1,0:T(8,128)}), f32[24,896]{1,0:T(8,128)}) %all-reduce.5.cloned.1.call-update) | async-done | bytes 86032 | tf_op jit(solution)/shard_map/psum | solution.py:49
  131.6 5.5 %convolution_bitcast_fusion = f32[3,32,8,128]{3,2,1,0:T(8,128)S(1)} fusion(bf16[4096,896]{1,0:T(8,128)(2,1)} %param.12, f32[24,896]{1,0:T(8,128)} %all-reduce.5.cloned.1.call-done, f32[24,896]{1,0:T(8,128)} %param.13), kind=kOutput, calls=%fused_computation.12 | convolution fusion | flops 176203776 | bytes 7905280 | tf_op jit(solution)/shard_map/qd,rd->qr/dot_general | solution.py:54
  137.1 0.8 copy.47
  137.9 0.0 all-reduce.7.cloned.1.call-update
  137.9 0.0 reduce-scatter.5.cloned.1.call-start
  138.0 1.7 convert.1
  139.7 54.9 %all-reduce.7.cloned.1.call-done = f32[24,32,128]{2,0,1:T(8,128)} async-done(((f32[24,32,128]{2,0,1:T(8,128)}), f32[24,32,128]{2,0,1:T(8,128)}) %all-reduce.7.cloned.1.call-update) | async-done | bytes 393232 | tf_op jit(solution)/shard_map/psum | solution.py:57
  194.6 1.4 fusion.12
  196.0 0.7 copy.33
  196.7 0.8 sub.24
  197.5 4.6 %fusion.5 = bf16[24,32,512]{2,0,1:T(8,128)(2,1)S(1)} fusion(bf16[32,512,128]{2,1,0:T(8,128)(2,1)} %param.11, f32[24,32,128]{2,0,1:T(8,128)} %all-reduce.7.cloned.1.call-done), kind=kOutput, calls=%fused_computation.11 | convolution fusion | flops 101154816 | bytes 5373952 | tf_op jit(solution)/shard_map/qhv,hcv->qhc/dot_general | solution.py:59
  202.1 0.0 copy-start.6
  202.1 0.0 copy-start.8
  202.1 0.2 copy.31
  202.3 0.4 copy-done.6
  202.8 0.0 copy-done.8
  202.8 0.8 fusion.6
  203.5 0.9 multiply_convert_fusion
  204.4 0.0 copy-start.1
  204.4 0.9 copy-done.1
  205.3 1.5 fusion.4
  206.8 0.0 reduce-scatter.5.cloned.1.call-update
  206.8 0.0 all-reduce.9.cloned.1.call-start
  206.9 3.2 %fusion.27 = f32[768,576]{1,0:T(8,128)} fusion(bf16[768,512]{0,1:T(8,128)(2,1)} %copy-done.1, bf16[512,576]{0,1:T(8,128)(2,1)S(1)} %copy-done.2), kind=kOutput, calls=%fused_computation.50 | convolution fusion | flops 452984832 | bytes 3145728 | tf_op jit(solution)/shard_map/dot_general | solution.py:72
  210.1 0.0 copy-start.3
  210.1 0.0 all-reduce.9.cloned.1.call-update
  210.1 0.9 copy-done.3
  211.0 0.0 copy-done.4
  211.0 0.6 multiply_reduce_fusion
  211.6 14.3 %psum.37 = f32[]{:T(128)} all-reduce(f32[]{:T(128)} %multiply_reduce_fusion), channel_id=1, replica_groups=mesh['heads'=4,'seq'=8] {'seq'}, use_global_device_ids=true, to_apply=%region_7.8 | all-reduce | flops 1 | bytes 8 | tf_op jit(solution)/shard_map/psum | solution.py:73
  226.6 4.8 %reduce-scatter.5.cloned.1.call-done = bf16[512,144]{0,1:T(8,128)(2,1)} async-done(((bf16[512,576]{0,1:T(8,128)(2,1)}), bf16[512,144]{0,1:T(8,128)(2,1)}) %reduce-scatter.5.cloned.1.call-update) | async-done | bytes 147472 | tf_op jit(solution)/shard_map/reduce_scatter | solution.py:84
  231.4 1.7 convert_element_type.51
  233.1 65.2 %all-reduce.9.cloned.1.call-done = f32[24,32,576]{2,1,0:T(8,128)} async-done(((f32[24,32,576]{2,1,0:T(8,128)}), f32[24,32,576]{2,1,0:T(8,128)}) %all-reduce.9.cloned.1.call-update) | async-done | bytes 1769488 | tf_op jit(solution)/shard_map/psum | solution.py:74
  298.3 0.6 copy.56
  298.9 2.9 copy.57
  (5 shorter events, 0.0 us)
Async XLA Ops:
  7.2 1.5 copy-start
  7.2 56.3 %reduce-scatter.3.cloned.1.call-start = ((), (), s32[]{:S(2)}) async-start(), calls=%async_computation.2 | async-start | bytes 1769472 | tf_op jit(solution)/shard_map/reduce_scatter | solution.py:34
  8.7 20.1 %copy-start.2 = (bf16[512,576]{0,1:T(8,128)(2,1)S(1)}, bf16[512,576]{0,1:T(8,128)(2,1)}, u32[]{:S(2)}) copy-start(bf16[512,576]{0,1:T(8,128)(2,1)} %param.8) | copy-start | bytes 1769476
  28.8 1.9 copy-start.5
  30.6 101.0 %all-reduce.5.cloned.1.call-start = ((), (), s32[]{:S(2)}) async-start(), calls=%async_computation.3 | async-start | bytes 172032 | tf_op jit(solution)/shard_map/psum | solution.py:49
  44.8 0.6 copy-start.7
  92.0 102.6 %all-reduce.7.cloned.1.call-start = ((), (), s32[]{:S(2)}) async-start(), calls=%async_computation.4 | async-start | bytes 786432 | tf_op jit(solution)/shard_map/psum | solution.py:57
  137.9 93.5 %reduce-scatter.5.cloned.1.call-start = ((), (), s32[]{:S(2)}) async-start(), calls=%async_computation.6 | async-start | bytes 737280 | tf_op jit(solution)/shard_map/reduce_scatter | solution.py:84
  202.1 0.7 copy-start.6
  202.1 0.7 copy-start.8
  204.4 0.9 copy-start.1
  206.8 91.4 %all-reduce.9.cloned.1.call-start = ((), (), s32[]{:S(2)}) async-start(), calls=%async_computation.5 | async-start | bytes 3932160 | tf_op jit(solution)/shard_map/psum | solution.py:74
  210.1 0.9 copy-start.3
  210.1 0.9 copy-start.4
Sparse Core Ops, SparseCore 0:
  30.8 32.6 reduce-scatter.2
  92.2 39.4 all-reduce.4
  138.0 56.5 all-reduce.6
  206.9 24.4 reduce-scatter.4
  234.2 63.9 all-reduce.8
where the time goes:
time: 310 us; the launch traced here: 309 us
  waiting for transfers between devices  174 us (56%)
  blocking collectives  61.3 us (20%)
  matrix products  30.8 us (10%)
  local copies, waits for them, and re-layouts  19.9 us (6%)
  between operations  15.7 us (5%)
  other arithmetic  7.67 us (2%)
    psum x1, waiting for transfers between devices, on_device(): query_sum = lax.psum(query_part, 'seq')  65.2 us
    psum x1, waiting for transfers between devices, on_device(): lax.psum(value_partial, 'seq').reshape(query_len, head_count, vwidth)  54.9 us
    psum x1, waiting for transfers between devices, on_device(): projected = lax.psum(partial_proj, 'heads')  39.5 us
    pmax x1, blocking collectives, on_device(): maximum = lax.pmax(local_top, 'seq')  18.1 us
    all_gather x1, blocking collectives, on_device(): lax.all_gather(share_value, 'seq', axis=0, tiled=True)  15.2 us
    psum x1, blocking collectives, on_device(): square_total = lax.psum(square_part, 'seq')  14.3 us
    psum x1, blocking collectives, on_device(): totals = lax.psum(jnp.sum(weights, axis=1), 'seq')  13.7 us
    reduce_scatter x1, waiting for transfers between devices, on_device(): lax.psum_scatter(partial_latent, 'seq', scatter_dimension=0, tiled=True)  9.28 us
  transfers between devices with their start and end apart: 5, of which 5 were waited for; matrix products, arithmetic and copies ran while one was open for 5% of the time, Pallas kernels for 0%

commit v1 on v0

v1 whole, which is shorter than its diff:
```python
import jax
import jax.numpy as jnp
from jax import lax
from jax.sharding import PartitionSpec as P

scale_factor = 0.07216878364870322
floor_value = -1e30
bf16 = jnp.bfloat16
f32 = jnp.float32


def stages_of(size, first=1):
    stages, stride = [], first
    while stride < size:
        left = size // stride
        radix = 4 if left % 4 == 0 else 2
        stages.append((stride, radix))
        stride *= radix
    return stages


def digit(axis, stage):
    stride, radix = stage
    return (lax.axis_index(axis) // stride) % radix


def swap(x, axis, stage, k):
    stride = stage[0]
    n = lax.axis_size(axis)
    return lax.ppermute(x, axis, [(i, i ^ (k * stride)) for i in range(n)])


def swap_all(x, axis, stage):
    got = {k: swap(x, axis, stage, k) for k in range(stage[1] - 1, 0, -1)}
    return [x] + [got[k] for k in range(1, stage[1])]


def pick(x, index):
    return lax.dynamic_index_in_dim(x, index, 0, keepdims=False)


def ordered(parts, d):
    stacked = jnp.stack(parts, 0)
    return jnp.stack([pick(stacked, d ^ j) for j in range(len(parts))], 0)


def scatter_sum(x, axis, stage):
    d = digit(axis, stage)
    got = {}
    for k in range(stage[1] - 1, 0, -1):
        got[k] = swap(pick(x, d ^ k), axis, stage, k)
    total = pick(x, d).astype(f32)
    for k in got:
        total = total + got[k].astype(f32)
    return total.astype(bf16)


def gather(x, axis, stage):
    return ordered(swap_all(x, axis, stage), digit(axis, stage))


def sum_all(x, axis, stage):
    parts = swap_all(x, axis, stage)
    total = parts[0].astype(f32)
    for p in parts[1:]:
        total = total + p.astype(f32)
    return total.astype(bf16)


def combine(parts):
    top = parts[0][1]
    for p in parts[1:]:
        top = jnp.maximum(top, p[1])
    mass = [p[2] * jnp.exp(p[1] - top) for p in parts]
    total = mass[0]
    for w in mass[1:]:
        total = total + w
    inverse = 1.0 / jnp.maximum(total, 1e-30)
    value = sum((w * inverse)[..., None] * p[0].astype(f32) for w, p in zip(mass, parts))
    return value.astype(bf16), top, total


def on_device(query, cache, segments, groups, value_up, out_proj, targets):
    query_len, head_count, width = query.shape
    latent, vwidth = value_up.shape[1], value_up.shape[2]
    rows = query_len * head_count
    cache_len = cache.shape[0]
    values = cache[:, :latent]
    seq_stages = stages_of(lax.axis_size("seq"), 2)
    head_stages = stages_of(lax.axis_size("heads"))
    pair = (1, 2)
    query_rows = jnp.transpose(query, (1, 0, 2)).reshape(rows, width)
    allowed = groups[:, None] == segments[None, :]
    allowed = jnp.broadcast_to(allowed[None], (head_count, query_len, cache_len)).reshape(rows, cache_len)
    scores = jnp.einsum("rc,tc->rt", query_rows, cache, preferred_element_type=f32) * scale_factor
    masked = jnp.where(allowed, scores, floor_value)
    local_top = jnp.max(masked, axis=1)
    weights = jnp.where(allowed, jnp.exp(masked - local_top[:, None]), 0.0)
    local_total = jnp.sum(weights, axis=1)
    mixed = jnp.dot(weights.astype(bf16), values, preferred_element_type=f32)
    mixed = (mixed / jnp.maximum(local_total, 1e-30)[:, None]).astype(bf16)
    value = jnp.einsum(
        "hqc,hcv->hqv",
        mixed.reshape(head_count, query_len, latent),
        value_up,
        preferred_element_type=f32,
    ).astype(bf16)
    half = head_count // 2
    value = value.reshape(2, half, query_len, vwidth)
    stats = jnp.stack([local_top, local_total], 0).reshape(2, 2, half, query_len)
    stats = jnp.transpose(stats, (1, 0, 2, 3))
    core = digit("seq", pair)
    got = (swap(pick(value, 1 - core), "seq", pair, 1), swap(pick(stats, 1 - core), "seq", pair, 1))
    own = (pick(value, core), pick(stats, core))
    state = combine([(v, s[0], s[1]) for v, s in (own, got)])
    for stage in seq_stages:
        vs = swap_all(state[0], "seq", stage)
        ss = swap_all(jnp.stack([state[1], state[2]], 0), "seq", stage)
        state = combine([(v, s[0], s[1]) for v, s in zip(vs, ss)])
    value_out = gather(state[0], "seq", pair).reshape(head_count, query_len, vwidth)
    stats = gather(jnp.stack([state[1], state[2]], 0), "seq", pair)
    top = stats[:, 0].reshape(rows)
    totals = stats[:, 1].reshape(rows)
    projected = jnp.einsum(
        "hqv,hvd->qd",
        value_out,
        out_proj.reshape(head_count, vwidth, out_proj.shape[1]),
        preferred_element_type=f32,
    )
    for stage in head_stages:
        parts = swap_all(projected, "heads", stage)
        d = digit("heads", stage)
        stacked = jnp.stack(parts, 0)
        projected = sum(pick(stacked, d ^ j) for j in range(stage[1]))
    residual = projected - targets
    square = jnp.sum(residual * residual).reshape(1, 1)
    model_width = targets.shape[1] * lax.axis_size("seq")
    d_projected = residual.astype(bf16)
    d_value = jnp.einsum(
        "qd,hvd->hqv",
        d_projected,
        out_proj.reshape(head_count, vwidth, out_proj.shape[1]),
        preferred_element_type=f32,
    ).astype(bf16)
    d_half = scatter_sum(d_value.reshape(2, half, query_len, vwidth), "seq", pair)
    for stage in seq_stages:
        d_half = sum_all(d_half, "seq", stage)
    d_value = gather(d_half, "seq", pair).reshape(head_count, query_len, vwidth)
    for stage in [pair] + seq_stages:
        parts = swap_all(square, "seq", stage)
        d = digit("seq", stage)
        stacked = jnp.stack(parts, 0)
        square = sum(pick(stacked, d ^ j) for j in range(stage[1]))
    loss = square[0, 0] / (query_len * model_width)
    d_latent = (
        jnp.einsum("hqv,hcv->hqc", d_value, value_up, preferred_element_type=f32)
        .astype(bf16)
        .reshape(rows, latent)
    )
    row_dot = jnp.sum(d_value.astype(f32) * value_out.astype(f32), axis=2).reshape(rows)
    factor = jnp.exp(local_top - top) / totals
    probs = weights * factor[:, None]
    d_probs = jnp.einsum("rc,tc->rt", d_latent, values, preferred_element_type=f32)
    d_scores = (scale_factor * probs * (d_probs - row_dot[:, None])).astype(bf16)
    query_part = jnp.dot(d_scores, cache, preferred_element_type=f32).astype(bf16)
    piece = query_part.reshape(2, rows // 2, width)
    piece = scatter_sum(piece, "seq", pair)
    for stage in seq_stages:
        piece = piece.reshape((stage[1], piece.shape[0] // stage[1], width))
        piece = scatter_sum(piece, "seq", stage)
    for stage in seq_stages[::-1]:
        piece = gather(piece, "seq", stage).reshape(-1, width)
    piece = gather(piece, "seq", pair).reshape(head_count, query_len, width)
    query_grad = jnp.transpose(piece, (1, 0, 2)).astype(f32)
    key_part = jnp.einsum("rt,rc->tc", d_scores, query_rows, preferred_element_type=f32)
    value_part = jnp.einsum("rt,rc->tc", probs.astype(bf16), d_latent, preferred_element_type=f32)
    cache_part = key_part + jnp.concatenate(
        [value_part, jnp.zeros((cache_len, width - latent), f32)], axis=1
    )
    cache_part = cache_part.astype(bf16)
    for stage in head_stages[::-1]:
        columns = cache_part.shape[1] // stage[1]
        pieces = jnp.stack([cache_part[:, j * columns : (j + 1) * columns] for j in range(stage[1])], 0)
        cache_part = scatter_sum(pieces, "heads", stage)
    return projected, loss, query_grad, cache_part.astype(f32)


def solution(mesh):
    in_specs = (
        P(None, "heads", None),
        P("seq", None),
        P("seq"),
        P(),
        P("heads", None, None),
        P("heads", "seq"),
        P(None, "seq"),
    )
    out_specs = (P(None, "seq"), P(), P(None, "heads", None), P("seq", "heads"))
    return jax.shard_map(
        on_device, mesh=mesh, in_specs=in_specs, out_specs=out_specs, check_vma=False
    )
```

time: 310 us -> 137 us (0.44)
  waiting for transfers between devices: 174 us -> 50.7 us
  blocking collectives: 61.3 us -> 0 us
  starting transfers between devices: 0.21 us -> 37.7 us
  matrix products: 30.8 us -> 18.4 us
  between operations: 15.7 us -> 6.26 us
  local copies, waits for them, and re-layouts: 19.9 us -> 12.3 us
  other arithmetic: 7.67 us -> 11.3 us
    psum x3 -> x0, waiting for transfers between devices: 160 us -> none  [the longest x1 65.2 us: on_device(): query_sum = lax.psum(query_part, 'seq')]
    ppermute x0 -> x33, waiting for transfers between devices: none -> 50.7 us  [swap(): return lax.ppermute(x, axis, [(i, i ^ k * stride) for i in range(n)])]
    ppermute x0 -> x33, starting transfers between devices: none -> 37.7 us  [swap(): return lax.ppermute(x, axis, [(i, i ^ k * stride) for i in range(n)])]
    psum x2 -> x0, blocking collectives: 28 us -> none  [the longest x1 14.3 us: on_device(): square_total = lax.psum(square_part, 'seq')]
    pmax x1 -> x0, blocking collectives: 18.1 us -> none  [on_device(): maximum = lax.pmax(local_top, 'seq')]
    all_gather x1 -> x0, blocking collectives: 15.2 us -> none  [on_device(): lax.all_gather(share_value, 'seq', axis=0, tiled=True)]
    reduce_scatter x2 -> x0, waiting for transfers between devices: 14.1 us -> none  [the longest x1 9.28 us: on_device(): lax.psum_scatter(partial_latent, 'seq', scatter_dimension=0, tiled=True)]
    dot_general x10, matrix products: 30.8 us -> 18.4 us  [the longest x1 4.53 us: on_device(): jnp.einsum('hqv,hcv->hqc', d_value, value_up, preferred_element_type=f32)]
  transfers between devices with their start and end apart: 5 -> 33, of which waited for: 5 -> 21; matrix products, arithmetic and copies ran while one was open for 5% -> 12% of each run, Pallas kernels for 0% -> 0%
where the time goes in v1:
time: 137 us
  waiting for transfers between devices  50.7 us (37%)
  starting transfers between devices  37.7 us (28%)
  matrix products  18.4 us (13%)
  local copies, waits for them, and re-layouts  12.3 us (9%)
  other arithmetic  11.3 us (8%)
  between operations  6.26 us (5%)
    ppermute x33, waiting for transfers between devices, swap(): return lax.ppermute(x, axis, [(i, i ^ k * stride) for i in range(n)])  50.7 us
    ppermute x33, starting transfers between devices, swap(): return lax.ppermute(x, axis, [(i, i ^ k * stride) for i in range(n)])  37.7 us
    another operation x4, other arithmetic, on_device(): stacked = jnp.stack(parts, 0)  5.58 us
    dynamic_slice x6, local copies, waits for them, and re-layouts, pick(): return lax.dynamic_index_in_dim(x, index, 0, keepdims=False)  4.82 us
    dot_general x1, matrix products, on_device(): jnp.einsum('hqv,hcv->hqc', d_value, value_up, preferred_element_type=f32)  4.53 us
    dot_general x1, matrix products, on_device(): jnp.einsum('hqv,hvd->qd', value_out, out_proj.reshape(head_count, vwidth,...  4.32 us
    unnamed x31, local copies, waits for them, and re-layouts  3.53 us
  transfers between devices with their start and end apart: 33, of which 21 were waited for; matrix products, arithmetic and copies ran while one was open for 12% of the time, Pallas kernels for 0%

profile of v1, /device:TPU:0, one launch (start us, length us, event | category | flops | bytes accessed | tf_op | source)
XLA Modules:
  0.0 136.7 jit_solution(12306822918596560782)
XLA Ops:
  0.7 0.8 broadcast_compare_fusion
  2.6 0.9 fusion.48
  4.7 1.8 %divide_convert_fusion = bf16[768,512]{1,0:T(8,128)(2,1)S(1)} fusion(f32[768]{0:T(1024)S(1)} %broadcast_maximum_fusion, bf16[512,576]{0,1:T(8,128)(2,1)} %param.8, pred[768,512]{0,1:T(32,128)(4,1)S(1)} %copy.21, f32[768,512]{0,1:T(8,128)S(1)} %get-tuple-element.64, f32[768]{0:T(1024)S(1)} %get-tuple-element.63), kind=kOutput, calls=%fused_computation.2 | convolution fusion | flops 404619264 | bytes 3282944 | tf_op jit(solution)/shard_map/dot_general | solution.py:100
  7.1 0.7 convolution_convert_fusion.3
  8.0 5.1 %collective-permute-start.3 = (f32[2,16,24]{2,1,0:T(8,128)S(1)}, f32[2,16,24]{2,1,0:T(8,128)S(1)}, u32[]{:S(2)}, u32[]{:S(2)}) collective-permute-start(f32[2,16,24]{2,1,0:T(8,128)S(1)} %pad_maximum_fusion.8), channel_id=1, source_target_pairs={{0,6},{1,7},{2,4},{3,5},{4,2},{5,3},{6,0},{7,1},{8,14},{9,15},{10,... | collective-permute-start | bytes 9224 | tf_op jit(solution)/shard_map/ppermute | solution.py:30
  13.1 0.6 collective-permute-start.1
  13.7 1.1 collective-permute-done.3
  14.8 2.9 %collective-permute-done.2 = f32[2,16,24]{2,1,0:T(8,128)S(1)} collective-permute-done((f32[2,16,24]{2,1,0:T(8,128)S(1)}, f32[2,16,24]{2,1,0:T(8,128)S(1)}, u32[]{:S(2)}, u32[]{:S(2)}) %collective-permute-start.2) | collective-permute-done | bytes 3104 | tf_op jit(solution)/shard_map/ppermute | solution.py:30
  18.0 1.5 %collective-permute-start.7 = (bf16[16,24,128]{2,1,0:T(8,128)(2,1)S(1)}, bf16[16,24,128]{2,1,0:T(8,128)(2,1)S(1)}, u32[]{:S(2)}, u32[]{:S(2)}) collective-permute-start(bf16[16,24,128]{2,1,0:T(8,128)(2,1)S(1)} %fusion.17), channel_id=1, source_target_pairs={{0,6},{1,7},{2,4},{3,5},{4,2},{5,3},{6,0},{7,1},{8,14},{9,15},{10,... | collective-permute-start | bytes 294920 | tf_op jit(solution)/shard_map/ppermute | solution.py:30
  19.5 0.6 collective-permute-start.6
  20.1 2.3 %collective-permute-start.5 = (bf16[16,24,128]{2,1,0:T(8,128)(2,1)S(1)}, bf16[16,24,128]{2,1,0:T(8,128)(2,1)S(1)}, u32[]{:S(2)}, u32[]{:S(2)}) collective-permute-start(bf16[16,24,128]{2,1,0:T(8,128)(2,1)S(1)} %fusion.17), channel_id=1, source_target_pairs={{0,2},{1,3},{2,0},{3,1},{4,6},{5,7},{6,4},{7,5},{8,10},{9,11},{10,... | collective-permute-start | bytes 294920 | tf_op jit(solution)/shard_map/ppermute | solution.py:30
  22.4 2.8 %collective-permute-done.7 = bf16[16,24,128]{2,1,0:T(8,128)(2,1)S(1)} collective-permute-done((bf16[16,24,128]{2,1,0:T(8,128)(2,1)S(1)}, bf16[16,24,128]{2,1,0:T(8,128)(2,1)S(1)}, u32[]{:S(2)}, u32[]{:S(2)}) %collective-permute-start.7) | collective-permute-done | bytes 98336 | tf_op jit(solution)/shard_map/ppermute | solution.py:30
  25.3 3.2 %collective-permute-done.6 = bf16[16,24,128]{2,1,0:T(8,128)(2,1)S(1)} collective-permute-done((bf16[16,24,128]{2,1,0:T(8,128)(2,1)S(1)}, bf16[16,24,128]{2,1,0:T(8,128)(2,1)S(1)}, u32[]{:S(2)}, u32[]{:S(2)}) %collective-permute-start.6) | collective-permute-done | bytes 98336 | tf_op jit(solution)/shard_map/ppermute | solution.py:30
  28.8 1.3 collective-permute-done.8
  30.2 4.3 %fusion.51 = f32[24,896,1]{1,0,2:T(8,128)S(1)} fusion(bf16[32,24,128]{2,1,0:T(8,128)(2,1)S(1)} %bitcast.236, bf16[32,128,896]{2,1,0:T(8,128)(2,1)} %bitcast.222), kind=kOutput, calls=%fused_computation.156 | convolution fusion | flops 176160768 | bytes 7622656 | tf_op jit(solution)/shard_map/hqv,hvd->qd/dot_general | solution.py:124
  34.5 1.6 %collective-permute-start.10 = (f32[24,896]{1,0:T(8,128)S(1)}, f32[24,896]{1,0:T(8,128)S(1)}, u32[]{:S(2)}, u32[]{:S(2)}) collective-permute-start(f32[24,896]{1,0:T(8,128)S(1)} %bitcast.249), channel_id=1, source_target_pairs={{0,16},{8,24},{16,0},{24,8},{1,17},{9,25},{17,1},{25,9},{2,18},{10... | collective-permute-start | bytes 258056 | tf_op jit(solution)/shard_map/ppermute | solution.py:30
  36.1 1.5 %collective-permute-start.9 = (f32[24,896]{1,0:T(8,128)S(1)}, f32[24,896]{1,0:T(8,128)S(1)}, u32[]{:S(2)}, u32[]{:S(2)}) collective-permute-start(f32[24,896]{1,0:T(8,128)S(1)} %bitcast.250), channel_id=1, source_target_pairs={{0,8},{8,0},{16,24},{24,16},{1,9},{9,1},{17,25},{25,17},{2,10},{10... | collective-permute-start | bytes 258056 | tf_op jit(solution)/shard_map/ppermute | solution.py:30
  38.1 1.1 collective-permute-done.10
  39.2 2.3 %collective-permute-done.9 = f32[24,896]{1,0:T(8,128)S(1)} collective-permute-done((f32[24,896]{1,0:T(8,128)S(1)}, f32[24,896]{1,0:T(8,128)S(1)}, u32[]{:S(2)}, u32[]{:S(2)}) %collective-permute-start.9) | collective-permute-done | bytes 86048 | tf_op jit(solution)/shard_map/ppermute | solution.py:30
  41.5 1.5 %collective-permute-done.11 = f32[24,896]{1,0:T(8,128)S(1)} collective-permute-done((f32[24,896]{1,0:T(8,128)S(1)}, f32[24,896]{1,0:T(8,128)S(1)}, u32[]{:S(2)}, u32[]{:S(2)}) %collective-permute-start.11) | collective-permute-done | bytes 86048 | tf_op jit(solution)/shard_map/ppermute | solution.py:30
  43.0 0.6 multiply_reduce_fusion.1
  43.7 2.3 %convolution_convert_fusion.2 = bf16[24,32,128]{2,0,1:T(8,128)(2,1)S(1)} fusion(bf16[32,128,896]{2,1,0:T(8,128)(2,1)S(1)} %bitcast.225, f32[24,896]{1,0:T(8,128)S(1)} %get-tuple-element.15, f32[24,896]{1,0:T(8,128)S(1)} %copy-done.8), kind=kOutput, calls=%fused_computation.10 | convolution fusion | flops 176302080 | bytes 7708672 | tf_op jit(solution)/shard_map/qd,hvd->hqv/dot_general | solution.py:139
  46.1 1.2 collective-permute-done.17
  47.4 2.0 %collective-permute-start.20 = (bf16[16,24,128]{2,1,0:T(8,128)(2,1)S(1)}, bf16[16,24,128]{2,1,0:T(8,128)(2,1)S(1)}, u32[]{:S(2)}, u32[]{:S(2)}) collective-permute-start(bf16[16,24,128]{2,1,0:T(8,128)(2,1)S(1)} %fusion.15), channel_id=1, source_target_pairs={{0,6},{1,7},{2,4},{3,5},{4,2},{5,3},{6,0},{7,1},{8,14},{9,15},{10,... | collective-permute-start | bytes 294920 | tf_op jit(solution)/shard_map/ppermute | solution.py:30
  49.4 2.5 %collective-permute-start.18 = (bf16[16,24,128]{2,1,0:T(8,128)(2,1)S(1)}, bf16[16,24,128]{2,1,0:T(8,128)(2,1)}, u32[]{:S(2)}, u32[]{:S(2)}) collective-permute-start(bf16[16,24,128]{2,1,0:T(8,128)(2,1)S(1)} %fusion.15), channel_id=1, source_target_pairs={{0,2},{1,3},{2,0},{3,1},{4,6},{5,7},{6,4},{7,5},{8,10},{9,11},{10,... | collective-permute-start | bytes 294920 | tf_op jit(solution)/shard_map/ppermute | solution.py:30
  52.1 3.0 %collective-permute-done.20 = bf16[16,24,128]{2,1,0:T(8,128)(2,1)S(1)} collective-permute-done((bf16[16,24,128]{2,1,0:T(8,128)(2,1)S(1)}, bf16[16,24,128]{2,1,0:T(8,128)(2,1)S(1)}, u32[]{:S(2)}, u32[]{:S(2)}) %collective-permute-start.20) | collective-permute-done | bytes 98336 | tf_op jit(solution)/shard_map/ppermute | solution.py:30
  55.0 3.3 %collective-permute-done.19 = bf16[16,24,128]{2,1,0:T(8,128)(2,1)S(1)} collective-permute-done((bf16[16,24,128]{2,1,0:T(8,128)(2,1)S(1)}, bf16[16,24,128]{2,1,0:T(8,128)(2,1)S(1)}, u32[]{:S(2)}, u32[]{:S(2)}) %collective-permute-start.19) | collective-permute-done | bytes 98336 | tf_op jit(solution)/shard_map/ppermute | solution.py:30
  58.4 0.9 add_convert_fusion
  59.4 1.3 collective-permute-done.21
  61.1 4.5 %convolution_convert_fusion.1 = bf16[32,24,512]{2,1,0:T(8,128)(2,1)S(1)} fusion(bf16[32,24,128]{2,1,0:T(8,128)(2,1)S(1)} %bitcast.240, bf16[32,512,128]{2,1,0:T(8,128)(2,1)} %param.11), kind=kOutput, calls=%fused_computation.8 | convolution fusion | flops 101056512 | bytes 5177344 | tf_op jit(solution)/shard_map/hqv,hcv->hqc/dot_general | solution.py:156
  65.6 0.9 multiply_convert_fusion
  66.5 0.9 copy-done.6
  67.4 1.5 %convolution_convert_fusion = bf16[768,576]{0,1:T(8,128)(2,1)} fusion(bf16[512,576]{0,1:T(8,128)(2,1)S(1)} %copy-done.11, bf16[768,512]{0,1:T(8,128)(2,1)S(1)} %multiply_convert_fusion), kind=kOutput, calls=%fused_computation.6 | convolution fusion | flops 453427200 | bytes 2260992 | tf_op jit(solution)/shard_map/dot_general | solution.py:165
  69.0 2.2 %reshape.392 = bf16[2,384,576]{1,0,2:T(2,128)(2,1)S(1)} reshape(bf16[768,576]{0,1:T(8,128)(2,1)} %convolution_convert_fusion) | data formatting | bytes 1769472 | tf_op jit(solution)/shard_map/reshape | solution.py:166
  71.2 1.8 %constant_dynamic-slice_fusion.5 = (bf16[1,384,576]{1,0,2:T(2,128)(2,1)S(1)}, bf16[1,384,576]{1,0,2:T(2,128)(2,1)S(1)}) fusion(bf16[2,384,576]{1,0,2:T(2,128)(2,1)S(1)} %reshape.392, s32[]{:T(128)S(6)} %select_n.129, s32[]{:T(128)S(6)} %select_n.131), kind=kLoop, calls=%fused_computation.101 | loop fusion | bytes 1769480 | tf_op jit(solution)/shard_map/jit(dynamic_index_in_dim)/dynamic_slice | solution.py:39
  73.3 0.8 fusion.2
  74.2 0.7 fusion
  75.4 2.0 %collective-permute-start.23 = (bf16[96,576]{1,0:T(8,128)(2,1)S(1)}, bf16[96,576]{1,0:T(8,128)(2,1)S(1)}, u32[]{:S(2)}, u32[]{:S(2)}) collective-permute-start(bf16[96,576]{1,0:T(8,128)(2,1)S(1)} %get-tuple-element.39), channel_id=1, source_target_pairs={{0,6},{1,7},{2,4},{3,5},{4,2},{5,3},{6,0},{7,1},{8,14},{9,15},{10,... | collective-permute-start | bytes 331784 | tf_op jit(solution)/shard_map/ppermute | solution.py:30
  77.4 2.5 %collective-permute-start.24 = (bf16[96,576]{1,0:T(8,128)(2,1)S(1)}, bf16[96,576]{1,0:T(8,128)(2,1)S(1)}, u32[]{:S(2)}, u32[]{:S(2)}) collective-permute-start(bf16[96,576]{1,0:T(8,128)(2,1)S(1)} %get-tuple-element.41), channel_id=1, source_target_pairs={{0,4},{1,5},{2,6},{3,7},{4,0},{5,1},{6,2},{7,3},{8,12},{9,13},{10,... | collective-permute-start | bytes 331784 | tf_op jit(solution)/shard_map/ppermute | solution.py:30
  79.9 3.6 %collective-permute-done.23 = bf16[96,576]{1,0:T(8,128)(2,1)S(1)} collective-permute-done((bf16[96,576]{1,0:T(8,128)(2,1)S(1)}, bf16[96,576]{1,0:T(8,128)(2,1)S(1)}, u32[]{:S(2)}, u32[]{:S(2)}) %collective-permute-start.23) | collective-permute-done | bytes 110624 | tf_op jit(solution)/shard_map/ppermute | solution.py:30
  83.5 3.9 %collective-permute-done.25 = bf16[96,576]{1,0:T(8,128)(2,1)S(1)} collective-permute-done((bf16[96,576]{1,0:T(8,128)(2,1)S(1)}, bf16[96,576]{1,0:T(8,128)(2,1)S(1)}, u32[]{:S(2)}, u32[]{:S(2)}) %collective-permute-start.25) | collective-permute-done | bytes 110624 | tf_op jit(solution)/shard_map/ppermute | solution.py:30
  87.4 1.1 collective-permute-done.24
  88.6 2.0 %collective-permute-start.28 = (bf16[96,576]{1,0:T(8,128)(2,1)S(1)}, bf16[96,576]{1,0:T(8,128)(2,1)S(1)}, u32[]{:S(2)}, u32[]{:S(2)}) collective-permute-start(bf16[96,576]{1,0:T(8,128)(2,1)S(1)} %fusion.14), channel_id=1, source_target_pairs={{0,6},{1,7},{2,4},{3,5},{4,2},{5,3},{6,0},{7,1},{8,14},{9,15},{10,... | collective-permute-start | bytes 331784 | tf_op jit(solution)/shard_map/ppermute | solution.py:30
  90.5 2.5 %collective-permute-start.26 = (bf16[96,576]{1,0:T(8,128)(2,1)S(1)}, bf16[96,576]{1,0:T(8,128)(2,1)S(1)}, u32[]{:S(2)}, u32[]{:S(2)}) collective-permute-start(bf16[96,576]{1,0:T(8,128)(2,1)S(1)} %fusion.14), channel_id=1, source_target_pairs={{0,2},{1,3},{2,0},{3,1},{4,6},{5,7},{6,4},{7,5},{8,10},{9,11},{10,... | collective-permute-start | bytes 331784 | tf_op jit(solution)/shard_map/ppermute | solution.py:30
  93.1 3.5 %collective-permute-done.28 = bf16[96,576]{1,0:T(8,128)(2,1)S(1)} collective-permute-done((bf16[96,576]{1,0:T(8,128)(2,1)S(1)}, bf16[96,576]{1,0:T(8,128)(2,1)S(1)}, u32[]{:S(2)}, u32[]{:S(2)}) %collective-permute-start.28) | collective-permute-done | bytes 110624 | tf_op jit(solution)/shard_map/ppermute | solution.py:30
  96.6 4.4 %collective-permute-done.27 = bf16[96,576]{1,0:T(8,128)(2,1)S(1)} collective-permute-done((bf16[96,576]{1,0:T(8,128)(2,1)S(1)}, bf16[96,576]{1,0:T(8,128)(2,1)S(1)}, u32[]{:S(2)}, u32[]{:S(2)}) %collective-permute-start.27) | collective-permute-done | bytes 110624 | tf_op jit(solution)/shard_map/ppermute | solution.py:30
  101.4 1.7 %collective-permute-start.30 = (bf16[512,144]{0,1:T(8,128)(2,1)S(1)}, bf16[512,144]{0,1:T(8,128)(2,1)S(1)}, u32[]{:S(2)}, u32[]{:S(2)}) collective-permute-start(bf16[512,144]{0,1:T(8,128)(2,1)S(1)} %get-tuple-element.28), channel_id=1, source_target_pairs={{0,24},{8,16},{16,8},{24,0},{1,25},{9,17},{17,9},{25,1},{2,26},{10... | collective-permute-start | bytes 442376 | tf_op jit(solution)/shard_map/ppermute | solution.py:30
  103.1 0.7 collective-permute-start.32
  103.8 1.1 collective-permute-start.31
  105.0 1.4 %collective-permute-done.12 = f32[1,1]{1,0:T(1,128)} collective-permute-done((f32[1,1]{1,0:T(1,128)}, f32[1,1]{1,0:T(1,128)}, u32[]{:S(2)}, u32[]{:S(2)}) %collective-permute-start.12) | collective-permute-done | bytes 36 | tf_op jit(solution)/shard_map/ppermute | solution.py:30
  106.4 1.2 constant_dynamic-slice_fusion.11
  107.5 1.2 constant_dynamic-slice_fusion.10
  108.7 1.8 %fusion.49 = f32[1,1,1]{2,1,0:T(1,128)} fusion(f32[1,1,1]{2,1,0:T(1,128)} %constant_dynamic-slice_fusion.11, s32[]{:T(128)S(6)} %select_n.129, f32[1,1,1]{2,1,0:T(1,128)} %bitcast.31), kind=kLoop, calls=%fused_computation.154 | loop fusion | flops 1 | bytes 16 | tf_op jit(solution)/shard_map/stack | solution.py:152
  110.5 1.8 %fusion.50 = f32[1,1,1]{2,1,0:T(1,128)} fusion(f32[1,1,1]{2,1,0:T(1,128)} %constant_dynamic-slice_fusion.10, s32[]{:T(128)S(6)} %select_n.131, f32[1,1,1]{2,1,0:T(1,128)} %bitcast.31), kind=kLoop, calls=%fused_computation.155 | loop fusion | flops 1 | bytes 16 | tf_op jit(solution)/shard_map/stack | solution.py:152
  113.6 3.3 %collective-permute-start.15 = (f32[1,1]{1,0:T(1,128)}, f32[1,1]{1,0:T(1,128)}, u32[]{:S(2)}, u32[]{:S(2)}) collective-permute-start(f32[1,1]{1,0:T(1,128)} %bitcast.35), channel_id=1, source_target_pairs={{0,6},{1,7},{2,4},{3,5},{4,2},{5,3},{6,0},{7,1},{8,14},{9,15},{10,... | collective-permute-start | bytes 20 | tf_op jit(solution)/shard_map/ppermute | solution.py:30
  116.9 2.3 %collective-permute-done.15 = f32[1,1]{1,0:T(1,128)} collective-permute-done((f32[1,1]{1,0:T(1,128)}, f32[1,1]{1,0:T(1,128)}, u32[]{:S(2)}, u32[]{:S(2)}) %collective-permute-start.15) | collective-permute-done | bytes 36 | tf_op jit(solution)/shard_map/ppermute | solution.py:30
  119.1 1.3 collective-permute-start.14
  120.4 3.1 %collective-permute-done.14 = f32[1,1]{1,0:T(1,128)} collective-permute-done((f32[1,1]{1,0:T(1,128)}, f32[1,1]{1,0:T(1,128)}, u32[]{:S(2)}, u32[]{:S(2)}) %collective-permute-start.14) | collective-permute-done | bytes 36 | tf_op jit(solution)/shard_map/ppermute | solution.py:30
  123.6 1.3 collective-permute-start.13
  124.9 2.4 %collective-permute-done.13 = f32[1,1]{1,0:T(1,128)} collective-permute-done((f32[1,1]{1,0:T(1,128)}, f32[1,1]{1,0:T(1,128)}, u32[]{:S(2)}, u32[]{:S(2)}) %collective-permute-start.13) | collective-permute-done | bytes 36 | tf_op jit(solution)/shard_map/ppermute | solution.py:30
  127.2 1.9 %pad_maximum_fusion.10 = f32[4,1,1]{0,2,1:T(1,128)S(1)} fusion(f32[1,1,1]{0,2,1:T(1,128)} %bitcast.40, f32[1,1,1]{0,2,1:T(1,128)} %bitcast.39, f32[1,1,1]{0,2,1:T(1,128)} %bitcast.37, f32[1,1,1]{0,2,1:T(1,128)} %bitcast.34), kind=kLoop, calls=%fused_computation.145 | loop fusion | flops 12 | bytes 32 | tf_op jit(solution)/shard_map/stack | solution.py:152
  129.2 0.6 constant_dynamic-slice_fusion.6
  132.4 0.8 fusion.18
  133.9 1.6 %copy.30 = f32[24,32,576]{2,1,0:T(8,128)} copy(f32[24,32,576]{2,0,1:T(8,128)S(1)} %convert_bitcast_fusion) | data formatting | bytes 3538944
  (103 shorter events, 7.1 us)
Async XLA Ops:
  0.6 1.5 %copy-start.5 = (bf16[24,32,576]{2,1,0:T(8,128)(2,1)S(1)}, bf16[24,32,576]{2,1,0:T(8,128)(2,1)}, u32[]{:S(2)}) copy-start(bf16[24,32,576]{2,1,0:T(8,128)(2,1)} %param.7) | copy-start | bytes 2654212
  1.5 1.1 copy-start.10
  2.1 63.5 %copy-start.1 = (pred[768,512]{0,1:T(32,128)(4,1)}, pred[768,512]{0,1:T(32,128)(4,1)S(1)}, u32[]{:S(2)}) copy-start(pred[768,512]{0,1:T(32,128)(4,1)S(1)} %copy.21) | copy-start | bytes 1179652
  4.1 3.8 %collective-permute-start = (f32[2,16,24]{2,1,0:T(8,128)S(1)}, f32[2,16,24]{2,1,0:T(8,128)S(1)}, u32[]{:S(2)}, u32[]{:S(2)}) collective-permute-start(f32[2,16,24]{2,1,0:T(8,128)S(1)} %get-tuple-element.51), channel_id=1, source_target_pairs={{0,1},{1,0},{2,3},{3,2},{4,5},{5,4},{6,7},{7,6},{8,9},{9,8},{10,11... | collective-permute-start | bytes 9224 | tf_op jit(solution)/shard_map/ppermute | solution.py:30
  4.7 2.3 %copy-start = (bf16[32,512,128]{2,1,0:T(8,128)(2,1)S(1)}, bf16[32,512,128]{2,1,0:T(8,128)(2,1)}, u32[]{:S(2)}) copy-start(bf16[32,512,128]{2,1,0:T(8,128)(2,1)} %param.11) | copy-start | bytes 12582916
  7.8 10.0 %collective-permute-start.4 = (bf16[16,24,128]{2,1,0:T(8,128)(2,1)S(1)}, bf16[16,24,128]{2,1,0:T(8,128)(2,1)S(1)}, u32[]{:S(2)}, u32[]{:S(2)}) collective-permute-start(bf16[16,24,128]{2,1,0:T(8,128)(2,1)S(1)} %dynamic-slice_bitcast_fusion.7), channel_id=1, source_target_pairs={{0,1},{1,0},{2,3},{3,2},{4,5},{5,4},{6,7},{7,6},{8,9},{9,8},{10,11... | collective-permute-start | bytes 294920 | tf_op jit(solution)/shard_map/ppermute | solution.py:30
  8.0 6.8 %collective-permute-start.3 = (f32[2,16,24]{2,1,0:T(8,128)S(1)}, f32[2,16,24]{2,1,0:T(8,128)S(1)}, u32[]{:S(2)}, u32[]{:S(2)}) collective-permute-start(f32[2,16,24]{2,1,0:T(8,128)S(1)} %pad_maximum_fusion.8), channel_id=1, source_target_pairs={{0,6},{1,7},{2,4},{3,5},{4,2},{5,3},{6,0},{7,1},{8,14},{9,15},{10,... | collective-permute-start | bytes 9224 | tf_op jit(solution)/shard_map/ppermute | solution.py:30
  13.1 4.6 %collective-permute-start.2 = (f32[2,16,24]{2,1,0:T(8,128)S(1)}, f32[2,16,24]{2,1,0:T(8,128)S(1)}, u32[]{:S(2)}, u32[]{:S(2)}) collective-permute-start(f32[2,16,24]{2,1,0:T(8,128)S(1)} %pad_maximum_fusion.8), channel_id=1, source_target_pairs={{0,4},{1,5},{2,6},{3,7},{4,0},{5,1},{6,2},{7,3},{8,12},{9,13},{10,... | collective-permute-start | bytes 9224 | tf_op jit(solution)/shard_map/ppermute | solution.py:30
  13.1 4.6 %collective-permute-start.1 = (f32[2,16,24]{2,1,0:T(8,128)S(1)}, f32[2,16,24]{2,1,0:T(8,128)S(1)}, u32[]{:S(2)}, u32[]{:S(2)}) collective-permute-start(f32[2,16,24]{2,1,0:T(8,128)S(1)} %pad_maximum_fusion.8), channel_id=1, source_target_pairs={{0,2},{1,3},{2,0},{3,1},{4,6},{5,7},{6,4},{7,5},{8,10},{9,11},{10,... | collective-permute-start | bytes 9224 | tf_op jit(solution)/shard_map/ppermute | solution.py:30
  18.0 7.3 %collective-permute-start.7 = (bf16[16,24,128]{2,1,0:T(8,128)(2,1)S(1)}, bf16[16,24,128]{2,1,0:T(8,128)(2,1)S(1)}, u32[]{:S(2)}, u32[]{:S(2)}) collective-permute-start(bf16[16,24,128]{2,1,0:T(8,128)(2,1)S(1)} %fusion.17), channel_id=1, source_target_pairs={{0,6},{1,7},{2,4},{3,5},{4,2},{5,3},{6,0},{7,1},{8,14},{9,15},{10,... | collective-permute-start | bytes 294920 | tf_op jit(solution)/shard_map/ppermute | solution.py:30
  19.5 8.9 %collective-permute-start.6 = (bf16[16,24,128]{2,1,0:T(8,128)(2,1)S(1)}, bf16[16,24,128]{2,1,0:T(8,128)(2,1)S(1)}, u32[]{:S(2)}, u32[]{:S(2)}) collective-permute-start(bf16[16,24,128]{2,1,0:T(8,128)(2,1)S(1)} %fusion.17), channel_id=1, source_target_pairs={{0,4},{1,5},{2,6},{3,7},{4,0},{5,1},{6,2},{7,3},{8,12},{9,13},{10,... | collective-permute-start | bytes 294920 | tf_op jit(solution)/shard_map/ppermute | solution.py:30
  20.1 8.3 %collective-permute-start.5 = (bf16[16,24,128]{2,1,0:T(8,128)(2,1)S(1)}, bf16[16,24,128]{2,1,0:T(8,128)(2,1)S(1)}, u32[]{:S(2)}, u32[]{:S(2)}) collective-permute-start(bf16[16,24,128]{2,1,0:T(8,128)(2,1)S(1)} %fusion.17), channel_id=1, source_target_pairs={{0,2},{1,3},{2,0},{3,1},{4,6},{5,7},{6,4},{7,5},{8,10},{9,11},{10,... | collective-permute-start | bytes 294920 | tf_op jit(solution)/shard_map/ppermute | solution.py:30
  28.7 1.4 collective-permute-start.8
  30.2 13.5 %slice-start = ((s8[7340032]{0:T(1024)(128)(4,1)}), s8[4194304]{0:T(1024)(128)(4,1)S(1)}, s32[]{:S(2)}) async-start(s8[7340032]{0:T(1024)(128)(4,1)} %bitcast.223), calls=%async_computation | async-start | bytes 8388608
  30.2 12.8 %copy-start.8 = (f32[24,896]{1,0:T(8,128)S(1)}, f32[24,896]{1,0:T(8,128)}, u32[]{:S(2)}) copy-start(f32[24,896]{1,0:T(8,128)} %param.13) | copy-start | bytes 258052
  30.2 13.5 %slice-start.1 = ((s8[7340032]{0:T(1024)(128)(4,1)}), s8[3145728]{0:T(1024)(128)(4,1)S(1)}, s32[]{:S(2)}) async-start(s8[7340032]{0:T(1024)(128)(4,1)} %bitcast.223), calls=%async_computation.1 | async-start | bytes 6291456
  34.5 4.7 %collective-permute-start.10 = (f32[24,896]{1,0:T(8,128)S(1)}, f32[24,896]{1,0:T(8,128)S(1)}, u32[]{:S(2)}, u32[]{:S(2)}) collective-permute-start(f32[24,896]{1,0:T(8,128)S(1)} %bitcast.249), channel_id=1, source_target_pairs={{0,16},{8,24},{16,0},{24,8},{1,17},{9,25},{17,1},{25,9},{2,18},{10... | collective-permute-start | bytes 258056 | tf_op jit(solution)/shard_map/ppermute | solution.py:30
  36.1 5.3 %collective-permute-start.9 = (f32[24,896]{1,0:T(8,128)S(1)}, f32[24,896]{1,0:T(8,128)S(1)}, u32[]{:S(2)}, u32[]{:S(2)}) collective-permute-start(f32[24,896]{1,0:T(8,128)S(1)} %bitcast.250), channel_id=1, source_target_pairs={{0,8},{8,0},{16,24},{24,16},{1,9},{9,1},{17,25},{25,17},{2,10},{10... | collective-permute-start | bytes 258056 | tf_op jit(solution)/shard_map/ppermute | solution.py:30
  37.6 5.4 %collective-permute-start.11 = (f32[24,896]{1,0:T(8,128)S(1)}, f32[24,896]{1,0:T(8,128)S(1)}, u32[]{:S(2)}, u32[]{:S(2)}) collective-permute-start(f32[24,896]{1,0:T(8,128)S(1)} %bitcast.251), channel_id=1, source_target_pairs={{0,24},{8,16},{16,8},{24,0},{1,25},{9,17},{17,9},{25,1},{2,26},{10... | collective-permute-start | bytes 258056 | tf_op jit(solution)/shard_map/ppermute | solution.py:30
  38.1 8.0 %collective-permute-start.16 = (f32[2,16,24]{2,1,0:T(8,128)S(1)}, f32[2,16,24]{2,1,0:T(8,128)S(1)}, u32[]{:S(2)}, u32[]{:S(2)}) collective-permute-start(f32[2,16,24]{2,1,0:T(8,128)S(1)} %get-tuple-element.52), channel_id=1, source_target_pairs={{0,1},{1,0},{2,3},{3,2},{4,5},{5,4},{6,7},{7,6},{8,9},{9,8},{10,11... | collective-permute-start | bytes 9224 | tf_op jit(solution)/shard_map/ppermute | solution.py:30
  43.7 2.3 %copy-start.9 = (f32[24,896]{1,0:T(8,128)}, f32[24,896]{1,0:T(8,128)S(1)}, u32[]{:S(2)}) copy-start(f32[24,896]{1,0:T(8,128)S(1)} %get-tuple-element.15) | copy-start | bytes 258052
  46.0 1.4 collective-permute-start.17
  47.4 7.6 %collective-permute-start.20 = (bf16[16,24,128]{2,1,0:T(8,128)(2,1)S(1)}, bf16[16,24,128]{2,1,0:T(8,128)(2,1)S(1)}, u32[]{:S(2)}, u32[]{:S(2)}) collective-permute-start(bf16[16,24,128]{2,1,0:T(8,128)(2,1)S(1)} %fusion.15), channel_id=1, source_target_pairs={{0,6},{1,7},{2,4},{3,5},{4,2},{5,3},{6,0},{7,1},{8,14},{9,15},{10,... | collective-permute-start | bytes 294920 | tf_op jit(solution)/shard_map/ppermute | solution.py:30
  49.4 8.9 %collective-permute-start.19 = (bf16[16,24,128]{2,1,0:T(8,128)(2,1)S(1)}, bf16[16,24,128]{2,1,0:T(8,128)(2,1)S(1)}, u32[]{:S(2)}, u32[]{:S(2)}) collective-permute-start(bf16[16,24,128]{2,1,0:T(8,128)(2,1)S(1)} %fusion.15), channel_id=1, source_target_pairs={{0,4},{1,5},{2,6},{3,7},{4,0},{5,1},{6,2},{7,3},{8,12},{9,13},{10,... | collective-permute-start | bytes 294920 | tf_op jit(solution)/shard_map/ppermute | solution.py:30
  49.4 8.9 %collective-permute-start.18 = (bf16[16,24,128]{2,1,0:T(8,128)(2,1)S(1)}, bf16[16,24,128]{2,1,0:T(8,128)(2,1)}, u32[]{:S(2)}, u32[]{:S(2)}) collective-permute-start(bf16[16,24,128]{2,1,0:T(8,128)(2,1)S(1)} %fusion.15), channel_id=1, source_target_pairs={{0,2},{1,3},{2,0},{3,1},{4,6},{5,7},{6,4},{7,5},{8,10},{9,11},{10,... | collective-permute-start | bytes 294920 | tf_op jit(solution)/shard_map/ppermute | solution.py:30
  59.3 1.4 collective-permute-start.21
  61.0 4.6 %copy-start.11 = (bf16[512,576]{0,1:T(8,128)(2,1)S(1)}, bf16[512,576]{0,1:T(8,128)(2,1)}, u32[]{:S(2)}) copy-start(bf16[512,576]{0,1:T(8,128)(2,1)} %param.8) | copy-start | bytes 1769476
  65.6 0.9 copy-start.3
  66.5 0.9 copy-start.6
  71.1 2.2 %copy-start.2 = (pred[768,512]{0,1:T(32,128)(4,1)S(1)}, pred[768,512]{0,1:T(32,128)(4,1)}, u32[]{:S(2)}) copy-start(pred[768,512]{0,1:T(32,128)(4,1)} %copy-done.1) | copy-start | bytes 1179652
  71.2 2.2 %copy-start.4 = (bf16[32,24,512]{2,1,0:T(8,128)(2,1)S(1)}, bf16[32,24,512]{2,1,0:T(8,128)(2,1)}, u32[]{:S(2)}) copy-start(bf16[32,24,512]{2,1,0:T(8,128)(2,1)} %copy-done.3) | copy-start | bytes 2359300
  73.1 1.1 copy-start.7
  73.1 1.9 %collective-permute-start.22 = (bf16[384,576]{0,1:T(8,128)(2,1)S(1)}, bf16[384,576]{0,1:T(8,128)(2,1)S(1)}, u32[]{:S(2)}, u32[]{:S(2)}) collective-permute-start(bf16[384,576]{0,1:T(8,128)(2,1)S(1)} %bitcast.246), channel_id=1, source_target_pairs={{0,1},{1,0},{2,3},{3,2},{4,5},{5,4},{6,7},{7,6},{8,9},{9,8},{10,11... | collective-permute-start | bytes 1327112 | tf_op jit(solution)/shard_map/ppermute | solution.py:30
  75.4 8.1 %collective-permute-start.23 = (bf16[96,576]{1,0:T(8,128)(2,1)S(1)}, bf16[96,576]{1,0:T(8,128)(2,1)S(1)}, u32[]{:S(2)}, u32[]{:S(2)}) collective-permute-start(bf16[96,576]{1,0:T(8,128)(2,1)S(1)} %get-tuple-element.39), channel_id=1, source_target_pairs={{0,6},{1,7},{2,4},{3,5},{4,2},{5,3},{6,0},{7,1},{8,14},{9,15},{10,... | collective-permute-start | bytes 331784 | tf_op jit(solution)/shard_map/ppermute | solution.py:30
  77.4 10.0 %collective-permute-start.25 = (bf16[96,576]{1,0:T(8,128)(2,1)S(1)}, bf16[96,576]{1,0:T(8,128)(2,1)S(1)}, u32[]{:S(2)}, u32[]{:S(2)}) collective-permute-start(bf16[96,576]{1,0:T(8,128)(2,1)S(1)} %get-tuple-element.40), channel_id=1, source_target_pairs={{0,2},{1,3},{2,0},{3,1},{4,6},{5,7},{6,4},{7,5},{8,10},{9,11},{10,... | collective-permute-start | bytes 331784 | tf_op jit(solution)/shard_map/ppermute | solution.py:30
  77.4 11.1 %collective-permute-start.24 = (bf16[96,576]{1,0:T(8,128)(2,1)S(1)}, bf16[96,576]{1,0:T(8,128)(2,1)S(1)}, u32[]{:S(2)}, u32[]{:S(2)}) collective-permute-start(bf16[96,576]{1,0:T(8,128)(2,1)S(1)} %get-tuple-element.41), channel_id=1, source_target_pairs={{0,4},{1,5},{2,6},{3,7},{4,0},{5,1},{6,2},{7,3},{8,12},{9,13},{10,... | collective-permute-start | bytes 331784 | tf_op jit(solution)/shard_map/ppermute | solution.py:30
  88.6 8.1 %collective-permute-start.28 = (bf16[96,576]{1,0:T(8,128)(2,1)S(1)}, bf16[96,576]{1,0:T(8,128)(2,1)S(1)}, u32[]{:S(2)}, u32[]{:S(2)}) collective-permute-start(bf16[96,576]{1,0:T(8,128)(2,1)S(1)} %fusion.14), channel_id=1, source_target_pairs={{0,6},{1,7},{2,4},{3,5},{4,2},{5,3},{6,0},{7,1},{8,14},{9,15},{10,... | collective-permute-start | bytes 331784 | tf_op jit(solution)/shard_map/ppermute | solution.py:30
  90.5 10.5 %collective-permute-start.27 = (bf16[96,576]{1,0:T(8,128)(2,1)S(1)}, bf16[96,576]{1,0:T(8,128)(2,1)S(1)}, u32[]{:S(2)}, u32[]{:S(2)}) collective-permute-start(bf16[96,576]{1,0:T(8,128)(2,1)S(1)} %fusion.14), channel_id=1, source_target_pairs={{0,4},{1,5},{2,6},{3,7},{4,0},{5,1},{6,2},{7,3},{8,12},{9,13},{10,... | collective-permute-start | bytes 331784 | tf_op jit(solution)/shard_map/ppermute | solution.py:30
  90.5 10.5 %collective-permute-start.26 = (bf16[96,576]{1,0:T(8,128)(2,1)S(1)}, bf16[96,576]{1,0:T(8,128)(2,1)S(1)}, u32[]{:S(2)}, u32[]{:S(2)}) collective-permute-start(bf16[96,576]{1,0:T(8,128)(2,1)S(1)} %fusion.14), channel_id=1, source_target_pairs={{0,2},{1,3},{2,0},{3,1},{4,6},{5,7},{6,4},{7,5},{8,10},{9,11},{10,... | collective-permute-start | bytes 331784 | tf_op jit(solution)/shard_map/ppermute | solution.py:30
  101.3 31.9 %collective-permute-start.29 = (bf16[384,576]{1,0:T(8,128)(2,1)S(1)}, bf16[384,576]{1,0:T(8,128)(2,1)S(1)}, u32[]{:S(2)}, u32[]{:S(2)}) collective-permute-start(bf16[384,576]{1,0:T(8,128)(2,1)S(1)} %bitcast.233), channel_id=1, source_target_pairs={{0,1},{1,0},{2,3},{3,2},{4,5},{5,4},{6,7},{7,6},{8,9},{9,8},{10,11... | collective-permute-start | bytes 1327112 | tf_op jit(solution)/shard_map/ppermute | solution.py:30
  101.4 31.0 %collective-permute-start.30 = (bf16[512,144]{0,1:T(8,128)(2,1)S(1)}, bf16[512,144]{0,1:T(8,128)(2,1)S(1)}, u32[]{:S(2)}, u32[]{:S(2)}) collective-permute-start(bf16[512,144]{0,1:T(8,128)(2,1)S(1)} %get-tuple-element.28), channel_id=1, source_target_pairs={{0,24},{8,16},{16,8},{24,0},{1,25},{9,17},{17,9},{25,1},{2,26},{10... | collective-permute-start | bytes 442376 | tf_op jit(solution)/shard_map/ppermute | solution.py:30
  103.1 29.3 %collective-permute-start.32 = (bf16[512,144]{0,1:T(8,128)(2,1)S(1)}, bf16[512,144]{0,1:T(8,128)(2,1)S(1)}, u32[]{:S(2)}, u32[]{:S(2)}) collective-permute-start(bf16[512,144]{0,1:T(8,128)(2,1)S(1)} %get-tuple-element.29), channel_id=1, source_target_pairs={{0,8},{8,0},{16,24},{24,16},{1,9},{9,1},{17,25},{25,17},{2,10},{10... | collective-permute-start | bytes 442376 | tf_op jit(solution)/shard_map/ppermute | solution.py:30
  103.8 28.6 %collective-permute-start.31 = (bf16[512,144]{0,1:T(8,128)(2,1)S(1)}, bf16[512,144]{0,1:T(8,128)(2,1)S(1)}, u32[]{:S(2)}, u32[]{:S(2)}) collective-permute-start(bf16[512,144]{0,1:T(8,128)(2,1)S(1)} %get-tuple-element.30), channel_id=1, source_target_pairs={{0,16},{8,24},{16,0},{24,8},{1,17},{9,25},{17,1},{25,9},{2,18},{10... | collective-permute-start | bytes 442376 | tf_op jit(solution)/shard_map/ppermute | solution.py:30
  105.0 1.4 %collective-permute-start.12 = (f32[1,1]{1,0:T(1,128)}, f32[1,1]{1,0:T(1,128)}, u32[]{:S(2)}, u32[]{:S(2)}) collective-permute-start(f32[1,1]{1,0:T(1,128)} %bitcast.32), channel_id=1, source_target_pairs={{0,1},{1,0},{2,3},{3,2},{4,5},{5,4},{6,7},{7,6},{8,9},{9,8},{10,11... | collective-permute-start | bytes 20 | tf_op jit(solution)/shard_map/ppermute | solution.py:30
  113.6 5.5 %collective-permute-start.15 = (f32[1,1]{1,0:T(1,128)}, f32[1,1]{1,0:T(1,128)}, u32[]{:S(2)}, u32[]{:S(2)}) collective-permute-start(f32[1,1]{1,0:T(1,128)} %bitcast.35), channel_id=1, source_target_pairs={{0,6},{1,7},{2,4},{3,5},{4,2},{5,3},{6,0},{7,1},{8,14},{9,15},{10,... | collective-permute-start | bytes 20 | tf_op jit(solution)/shard_map/ppermute | solution.py:30
  119.1 4.4 %collective-permute-start.14 = (f32[1,1]{1,0:T(1,128)}, f32[1,1]{1,0:T(1,128)}, u32[]{:S(2)}, u32[]{:S(2)}) collective-permute-start(f32[1,1]{1,0:T(1,128)} %bitcast.35), channel_id=1, source_target_pairs={{0,4},{1,5},{2,6},{3,7},{4,0},{5,1},{6,2},{7,3},{8,12},{9,13},{10,... | collective-permute-start | bytes 20 | tf_op jit(solution)/shard_map/ppermute | solution.py:30
  123.6 3.7 %collective-permute-start.13 = (f32[1,1]{1,0:T(1,128)}, f32[1,1]{1,0:T(1,128)}, u32[]{:S(2)}, u32[]{:S(2)}) collective-permute-start(f32[1,1]{1,0:T(1,128)} %bitcast.35), channel_id=1, source_target_pairs={{0,2},{1,3},{2,0},{3,1},{4,6},{5,7},{6,4},{7,5},{8,10},{9,11},{10,... | collective-permute-start | bytes 20 | tf_op jit(solution)/shard_map/ppermute | solution.py:30

commit v2 on v1

v2 whole, which is shorter than its diff:
```python
import functools

import jax
import jax.numpy as jnp
from jax import lax
from jax.experimental import pallas as pl
from jax.experimental.pallas import tpu as pltpu
from jax.sharding import PartitionSpec as P

scale_factor = 0.07216878364870322
floor_value = -1e30
tiny = 1e-30
lanes = 128
waiting = 8_000_000_000
bf16 = jnp.bfloat16
f32 = jnp.float32
NT = (((1,), (1,)), ((), ()))


def stages_of(size, first=1):
    stages, stride = [], first
    while stride < size:
        left = size // stride
        radix = 4 if left % 4 == 0 else 2
        stages.append((stride, radix))
        stride *= radix
    return stages


def digit(axis, stage):
    stride, radix = stage
    return (lax.axis_index(axis) // stride) % radix


def swap(x, axis, stage, k):
    stride = stage[0]
    n = lax.axis_size(axis)
    return lax.ppermute(x, axis, [(i, i ^ (k * stride)) for i in range(n)])


def swap_all(x, axis, stage):
    got = {k: swap(x, axis, stage, k) for k in range(stage[1] - 1, 0, -1)}
    return [x] + [got[k] for k in range(1, stage[1])]


def pick(x, index):
    return lax.dynamic_index_in_dim(x, index, 0, keepdims=False)


def ordered(parts, d):
    stacked = jnp.stack(parts, 0)
    return jnp.stack([pick(stacked, d ^ j) for j in range(len(parts))], 0)


def scatter_sum(x, axis, stage):
    d = digit(axis, stage)
    got = {}
    for k in range(stage[1] - 1, 0, -1):
        got[k] = swap(pick(x, d ^ k), axis, stage, k)
    total = pick(x, d).astype(f32)
    for k in got:
        total = total + got[k].astype(f32)
    return total.astype(bf16)


def gather(x, axis, stage):
    return ordered(swap_all(x, axis, stage), digit(axis, stage))


def call(kernel, out_shape, *args, scratch=(), specs=None, flops=0, grant=4 << 20):
    moved = sum(a.size * a.dtype.itemsize for a in args)
    vmem = pl.BlockSpec(memory_space=pltpu.VMEM)
    return pl.pallas_call(
        kernel,
        out_shape=out_shape,
        in_specs=specs or [vmem] * len(args),
        out_specs=jax.tree.map(lambda _: vmem, out_shape),
        scratch_shapes=list(scratch),
        cost_estimate=pl.CostEstimate(flops=flops, bytes_accessed=moved, transcendentals=0),
        compiler_params=pltpu.CompilerParams(vmem_limit_bytes=grant),
    )(*args)


def split3(x):
    high = x.astype(bf16).astype(f32)
    rest = x - high
    middle = rest.astype(bf16).astype(f32)
    return high, middle, (rest - middle).astype(bf16).astype(f32)


def pack(top, total, heads):
    slab = jnp.zeros(top.shape, f32)
    for i, part in enumerate(split3(top) + split3(total)):
        slab = slab + (pltpu.roll(part, i * heads, 1) if i else part)
    return slab.astype(bf16)


def unpack(slab, heads):
    x = slab.astype(f32)
    s = x + pltpu.roll(x, lanes - heads, 1) + pltpu.roll(x, lanes - 2 * heads, 1)
    keep = lax.broadcasted_iota(jnp.int32, x.shape, 1) < heads
    top = jnp.where(keep, s, 0.0)
    total = jnp.where(keep, pltpu.roll(s, lanes - 3 * heads, 1), 0.0)
    return top, total


def choose(first, a, b):
    return jnp.where(first, a.astype(f32), b.astype(f32))


def forward_kernel(q_ref, cache_ref, seg_ref, grp_ref, up_hbm, own_ref, other_ref, w_ref, stat_ref, rows_ref, up_ref, mix_ref, pay_ref, sem):
    head_count, latent, _ = up_ref.shape
    query_len = grp_ref.shape[0]
    half = head_count // 2
    block = half // 2
    load = pltpu.make_async_copy(up_hbm, up_ref, sem)
    load.start()
    allowed = grp_ref[...] == seg_ref[...]
    lane = lax.broadcasted_iota(jnp.int32, (query_len, lanes), 1)
    zero = jnp.zeros((query_len, lanes), f32)
    grid = (query_len, query_len * head_count)
    offset = lax.broadcasted_iota(jnp.int32, grid, 1) - head_count * lax.broadcasted_iota(jnp.int32, grid, 0)
    stats = [[zero, zero], [zero, zero]]
    for b in range(head_count // block):
        first = b * block * query_len
        size = block * query_len
        take = [jnp.where(offset == b * block + j, 1.0, 0.0).astype(bf16) for j in range(block)]
        moved = jnp.dot(jnp.concatenate(take, axis=0), q_ref[...], preferred_element_type=f32).astype(bf16)
        rows_ref[first : first + size, :] = moved
        scores = lax.dot_general(moved, cache_ref[...], NT, preferred_element_type=f32)
        inverse = []
        for j in range(block):
            h = b * block + j
            p, at = divmod(h, half)
            s = jnp.where(allowed, scores[j * query_len : (j + 1) * query_len, :] * scale_factor, floor_value)
            top = jnp.max(s, axis=1, keepdims=True)
            w = jnp.where(allowed, jnp.exp(s - top), 0.0)
            total = jnp.sum(w, axis=1, keepdims=True)
            w_ref[h * query_len : (h + 1) * query_len, :] = w
            stats[p][0] = jnp.where(lane == at, top, stats[p][0])
            stats[p][1] = jnp.where(lane == at, total, stats[p][1])
            inverse.append(1.0 / jnp.maximum(total, tiny))
        mixed = jnp.dot(
            w_ref[first : first + size, :].astype(bf16), cache_ref[:, :latent], preferred_element_type=f32
        )
        for j in range(block):
            mix_ref[b * block + j] = (mixed[j * query_len : (j + 1) * query_len, :] * inverse[j]).astype(bf16)
    for p in range(2):
        stat_ref[p, 0] = stats[p][0]
        stat_ref[p, 1] = stats[p][1]
        pay_ref[p, half] = pack(stats[p][0], stats[p][1], half)
    load.wait()
    for h in range(head_count):
        p, at = divmod(h, half)
        pay_ref[p, at] = jnp.dot(mix_ref[h], up_ref[h], preferred_element_type=f32).astype(bf16)
    core = lax.axis_index("seq") % 2
    own_ref[...] = pay_ref[core]
    other_ref[...] = pay_ref[1 - core]


def combine_kernel(*refs):
    parts, out_ref = refs[:-1], refs[-1]
    heads = out_ref.shape[0] - 1
    stats = [unpack(r[heads], heads) for r in parts]
    top = functools.reduce(jnp.maximum, [s[0] for s in stats])
    mass = [s[1] * jnp.exp(s[0] - top) for s in stats]
    total = functools.reduce(jnp.add, mass)
    inverse = 1.0 / jnp.maximum(total, tiny)
    share = [m * inverse for m in mass]
    for h in range(heads):
        v = share[0][:, h : h + 1] * parts[0][h].astype(f32)
        for s, r in zip(share[1:], parts[1:]):
            v = v + s[:, h : h + 1] * r[h].astype(f32)
        out_ref[h] = v.astype(bf16)
    out_ref[heads] = pack(top, total, heads)


def in_order(parts, d, index=None):
    vals = [(r[...] if index is None else r[index]).astype(f32) for r in parts]
    out = []
    for j in range(len(parts)):
        k = d ^ j
        v = vals[0]
        for i in range(1, len(parts)):
            v = jnp.where(k == i, vals[i], v)
        out.append(v)
    return out


def project_kernel(val_ref, val_got_ref, proj_ref, part_ref, row_ref):
    half = val_ref.shape[0] - 1
    vwidth = val_ref.shape[2]
    low = lax.axis_index("seq") % 2 == 0
    for at in range(half):
        a = choose(low, val_ref[at], val_got_ref[at]).astype(bf16)
        b = choose(low, val_got_ref[at], val_ref[at]).astype(bf16)
        row_ref[:, at * vwidth : (at + 1) * vwidth] = a
        row_ref[:, (half + at) * vwidth : (half + at + 1) * vwidth] = b
    total = jnp.zeros(part_ref.shape, f32)
    depth = proj_ref.shape[0]
    step = 4 * vwidth if half % 2 == 0 else 2 * vwidth
    for k in range(0, depth, step):
        total = total + jnp.dot(row_ref[:, k : k + step], proj_ref[k : k + step, :], preferred_element_type=f32)
    part_ref[...] = total.astype(bf16)


def residual_kernel(stage, *refs):
    parts, (target_ref, w_ref, proj_ref, own_ref, other_ref, pay_ref) = refs[:-6], refs[-6:]
    projected = functools.reduce(jnp.add, in_order(parts, digit("heads", stage)))
    proj_ref[...] = projected
    residual = projected - target_ref[...]
    square = residual * residual
    rows, columns = square.shape
    tile = jnp.zeros((8, lanes), f32)
    for i in range(rows // 8):
        for j in range(columns // lanes):
            tile = tile + square[i * 8 : (i + 1) * 8, j * lanes : (j + 1) * lanes]
        if columns % lanes:
            left = square[i * 8 : (i + 1) * 8, columns - columns % lanes :]
            tile = tile + jnp.concatenate([left, jnp.zeros((8, lanes - columns % lanes), f32)], axis=1)
    half, vwidth = pay_ref.shape[1] - 1, pay_ref.shape[3]
    slab = jnp.concatenate(split3(tile), axis=0).astype(bf16)
    d_projected = residual.astype(bf16)
    group = 4 if half % 4 == 0 else 1
    for p in range(2):
        pay_ref[p, half] = slab
        for at in range(0, half, group):
            first = (p * half + at) * vwidth
            d = lax.dot_general(
                d_projected, w_ref[first : first + group * vwidth, :], NT, preferred_element_type=f32
            )
            for j in range(group):
                pay_ref[p, at + j] = d[:, j * vwidth : (j + 1) * vwidth].astype(bf16)
    core = lax.axis_index("seq") % 2
    own_ref[...] = pay_ref[core]
    other_ref[...] = pay_ref[1 - core]


def partial_sum_kernel(*refs):
    parts, out_ref = refs[:-1], refs[-1]
    total = parts[0][...].astype(f32)
    for r in parts[1:]:
        total = total + r[...].astype(f32)
    out_ref[...] = total.astype(bf16)


def sum_kernel(stage, *refs):
    parts, out_ref = refs[:-1], refs[-1]
    last = out_ref.shape[0] - 1
    for h in range(last):
        total = parts[0][h].astype(f32)
        for r in parts[1:]:
            total = total + r[h].astype(f32)
        out_ref[h] = total.astype(bf16)
    tiles = [s[:8] + s[8:16] + s[16:24] for s in in_order(parts, digit("seq", stage), last)]
    out_ref[last] = jnp.concatenate(split3(functools.reduce(jnp.add, tiles)), axis=0).astype(bf16)


def backward_kernel(chunk, dv_ref, dv_got_ref, val_ref, val_got_ref, w_ref, stat_ref, cache_ref, up_ref, qg_ref, ds_ref, probs_ref, dl_ref):
    _, latent, _ = up_ref.shape
    half = dv_ref.shape[0] - 1
    query_len = dv_ref.shape[1]
    count = ds_ref.shape[0]
    width = cache_ref.shape[1]
    block = 8
    low = lax.axis_index("seq") % 2 == 0
    own_stats = unpack(val_ref[half], half)
    got_stats = unpack(val_got_ref[half], half)
    factors = []
    for p in range(2):
        mine = low if p == 0 else jnp.logical_not(low)
        top = jnp.where(mine, own_stats[0], got_stats[0])
        total = jnp.where(mine, own_stats[1], got_stats[1])
        factors.append(jnp.exp(stat_ref[p, 0] - top) / jnp.maximum(total, tiny))
    size = block * query_len
    grid = (block, size)
    offset = lax.broadcasted_iota(jnp.int32, grid, 1) - query_len * lax.broadcasted_iota(jnp.int32, grid, 0)
    take = [jnp.where(offset == q, 1.0, 0.0).astype(bf16) for q in range(query_len)]
    turn = jnp.concatenate(take, axis=0)
    span = query_len // 4
    lines = span * block
    full = width - width % lanes
    for b in range(count // block):
        dots = []
        for j in range(block):
            n = b * block + j
            h = chunk * count + n
            p, at = divmod(h, half)
            mine = low if p == 0 else jnp.logical_not(low)
            dv = choose(mine, dv_ref[at], dv_got_ref[at])
            val = choose(mine, val_ref[at], val_got_ref[at])
            dots.append(jnp.sum(dv * val, axis=1, keepdims=True))
            dl = lax.dot_general(dv.astype(bf16), up_ref[h], NT, preferred_element_type=f32)
            dl_ref[n] = dl.astype(bf16)
        dlb = dl_ref[b * block : (b + 1) * block].reshape(size, latent)
        d_probs = lax.dot_general(dlb, cache_ref[:, :latent], NT, preferred_element_type=f32)
        for j in range(block):
            n = b * block + j
            h = chunk * count + n
            p, at = divmod(h, half)
            rows = slice(h * query_len, (h + 1) * query_len)
            probs = w_ref[rows, :] * factors[p][:, at : at + 1]
            probs_ref[n] = probs.astype(bf16)
            d = d_probs[j * query_len : (j + 1) * query_len, :] - dots[j]
            ds_ref[n] = (scale_factor * probs * d).astype(bf16)
        dsb = ds_ref[b * block : (b + 1) * block].reshape(size, cache_ref.shape[0])
        qg = jnp.dot(dsb, cache_ref[...], preferred_element_type=f32).astype(bf16)
        qg = jnp.dot(turn, qg, preferred_element_type=f32)
        for g in range(4):
            x = qg[g * lines : (g + 1) * lines, :]
            to = qg_ref.at[g // 2, b * 2 + g % 2]
            for c in range(full // lanes):
                to[c * lines : (c + 1) * lines, :] = x[:, c * lanes : (c + 1) * lanes].astype(bf16)
            last = jnp.concatenate([x[: lines // 2, full:], x[lines // 2 :, full:]], axis=1)
            to[(full // lanes) * lines :, :] = last.astype(bf16)


def final_kernel(stage, chunks, *refs):
    out_ref = refs[-1]
    count = stage[1]
    core = lax.axis_index("seq") % 2
    d = digit("seq", stage)
    query_len, _, width = out_ref.shape
    block = 8
    span = query_len // 4
    lines = span * block
    full = width - width % lanes
    left = width - full
    unit = lines * width // lanes
    at = 0
    for chunk in range(chunks):
        for half in (core, 1 - core):
            for k in range(count):
                ref = refs[at]
                at += 1
                held = ref.shape[0] // unit
                for u in range(held):
                    index = (d ^ k) * held + u
                    first = half * 2 * span + lax.rem(index, 2) * span
                    head = pl.multiple_of((chunk * held * count // 2 + index // 2) * block, block)
                    for q in range(span):
                        to = out_ref.at[first + q, pl.ds(head, block), :]
                        for c in range(full // lanes):
                            line = u * unit + c * lines + q * block
                            to[:, c * lanes : (c + 1) * lanes] = ref[line : line + block, :].astype(f32)
                        far = q * block >= lines // 2
                        line = u * unit + (full // lanes) * lines + q * block - (lines // 2 if far else 0)
                        x = ref[line : line + block, :].astype(f32)
                        to[:, full:] = x[:, left:] if far else x[:, :left]


def on_device(query, cache, segments, groups, value_up, out_proj, targets):
    query_len, head_count, width = query.shape
    latent, vwidth = value_up.shape[1], value_up.shape[2]
    rows = query_len * head_count
    cache_len = cache.shape[0]
    half = head_count // 2
    seq_stages = stages_of(lax.axis_size("seq"), 2)
    head_stages = stages_of(lax.axis_size("heads"))
    pair = (1, 2)
    shape = jax.ShapeDtypeStruct
    vmem = pl.BlockSpec(memory_space=pltpu.VMEM)
    payload = shape((half + 1, query_len, vwidth), bf16)
    hbm = pl.BlockSpec(memory_space=pltpu.HBM)
    own, other, weights, stats, query_rows = call(
        forward_kernel,
        (
            payload,
            payload,
            shape((rows, cache_len), f32),
            shape((2, 2, query_len, lanes), f32),
            shape((rows, width), bf16),
        ),
        query.reshape(rows, width),
        cache,
        segments.reshape(1, cache_len),
        groups.reshape(query_len, 1),
        value_up,
        scratch=(
            pltpu.VMEM(value_up.shape, bf16),
            pltpu.VMEM((head_count, query_len, latent), bf16),
            pltpu.VMEM((2, half + 1, query_len, vwidth), bf16),
            pltpu.SemaphoreType.DMA,
        ),
        specs=[vmem] * 4 + [hbm],
        flops=2 * rows * (cache_len * (width + latent) + latent * vwidth),
        grant=46 << 20,
    )
    state = call(combine_kernel, payload, own, swap(other, "seq", pair, 1))
    for stage in seq_stages:
        state = call(combine_kernel, payload, *swap_all(state, "seq", stage), flops=waiting)
    state_got = swap(state, "seq", pair, 1)
    partial = call(
        project_kernel,
        shape(targets.shape, bf16),
        state,
        state_got,
        out_proj,
        scratch=(pltpu.VMEM((query_len, head_count * vwidth), bf16),),
        flops=2 * query_len * out_proj.size,
    )
    for stage in head_stages[:-1]:
        partial = call(partial_sum_kernel, shape(partial.shape, bf16), *swap_all(partial, "heads", stage))
    projected, own, other = call(
        functools.partial(residual_kernel, head_stages[-1]),
        (shape(targets.shape, f32), payload, payload),
        *swap_all(partial, "heads", head_stages[-1]),
        targets,
        out_proj,
        scratch=(pltpu.VMEM((2, half + 1, query_len, vwidth), bf16),),
        flops=2 * query_len * out_proj.size,
    )
    d_state = call(functools.partial(sum_kernel, pair), payload, own, swap(other, "seq", pair, 1))
    for stage in seq_stages:
        d_state = call(functools.partial(sum_kernel, stage), payload, *swap_all(d_state, "seq", stage), flops=waiting)
    d_got = swap(d_state, "seq", pair, 1)
    loss = jnp.sum(d_state[half].astype(f32)) / (query_len * targets.shape[1] * lax.axis_size("seq"))
    chunks = 1
    count = head_count // chunks
    units = shape((2, count // 4, query_len // 4 * 8 * width // lanes, lanes), bf16)
    wide = shape((count, query_len, cache_len), bf16)
    local = [
        call(
            functools.partial(backward_kernel, chunk),
            (units, wide, wide, shape((count, query_len, latent), bf16)),
            d_state,
            d_got,
            state,
            state_got,
            weights,
            stats,
            cache,
            value_up,
            flops=rows * (cache_len * (width + latent) + latent * vwidth),
            grant=10 << 20,
        )
        for chunk in range(chunks)
    ]
    pieces = [scatter_sum(x[0].reshape(2, -1, lanes), "seq", pair) for x in local]
    for stage in seq_stages:
        pieces = [scatter_sum(x.reshape(stage[1], -1, lanes), "seq", stage) for x in pieces]
    cache_part = None
    for chunk, (_, d_scores, probs, d_latent) in enumerate(local):
        d_scores = d_scores.reshape(-1, cache_len)
        span = query_rows.shape[0] // chunks
        held = query_rows[chunk * span : (chunk + 1) * span]
        key_part = jnp.einsum("rt,rc->ct", d_scores, held, preferred_element_type=f32)
        value_part = jnp.einsum(
            "rt,rc->ct", probs.reshape(-1, cache_len), d_latent.reshape(-1, latent), preferred_element_type=f32
        )
        part = jnp.concatenate([key_part[:latent] + value_part, key_part[latent:]], axis=0)
        cache_part = part if cache_part is None else cache_part + part
    cache_part = cache_part.astype(bf16)
    for stage in head_stages[::-1]:
        cache_part = cache_part.reshape(stage[1], cache_part.shape[0] // stage[1], cache_len)
        cache_part = scatter_sum(cache_part, "heads", stage)
    for stage in seq_stages[:0:-1]:
        pieces = [gather(x, "seq", stage).reshape(-1, lanes) for x in pieces]
    parts = []
    for x in pieces:
        own = swap_all(x, "seq", seq_stages[0])
        parts += own + [swap(p, "seq", pair, 1) for p in own]
    query_grad = call(
        functools.partial(final_kernel, seq_stages[0], chunks), shape(query.shape, f32), *parts
    )
    return projected, loss, query_grad, cache_part.T.astype(f32)


def solution(mesh):
    in_specs = (
        P(None, "heads", None),
        P("seq", None),
        P("seq"),
        P(),
        P("heads", None, None),
        P("heads", "seq"),
        P(None, "seq"),
    )
    out_specs = (P(None, "seq"), P(), P(None, "heads", None), P("seq", "heads"))

    return jax.shard_map(on_device, mesh=mesh, in_specs=in_specs, out_specs=out_specs, check_vma=False)
```

time: 137 us -> 91 us (0.66)
  matrix products: 18.4 us -> 1.25 us
  Pallas kernels: 0 us -> 15.8 us
  waiting for transfers between devices: 50.7 us -> 37.7 us
  starting transfers between devices: 37.7 us -> 26.8 us
  other arithmetic: 11.3 us -> 1.61 us
  local copies, waits for them, and re-layouts: 12.3 us -> 4.8 us
  between operations: 6.26 us -> 2.73 us
    dot_general x10 -> x2, matrix products: 18.4 us -> 1.25 us  [the longest x1 0.65 us: on_device(): jnp.einsum('rt,rc->ct', d_scores, held, preferred_element_type=f32)]
    pallas_call x0 -> x9, Pallas kernels: none -> 15.8 us  [call(): pl.pallas_call(kernel, out_shape=out_shape, in_specs=specs or [vmem] * le...]
    ppermute x33 -> x27, waiting for transfers between devices: 50.7 us -> 37.7 us  [swap(): return lax.ppermute(x, axis, [(i, i ^ k * stride) for i in range(n)])]
    ppermute x33 -> x27, starting transfers between devices: 37.7 us -> 26.8 us  [swap(): return lax.ppermute(x, axis, [(i, i ^ k * stride) for i in range(n)])]
    another operation x17 -> x0, other arithmetic: 6.68 us -> none  [the longest x4 5.58 us: on_device(): stacked = jnp.stack(parts, 0)]
    dynamic_slice x6 -> x0, local copies, waits for them, and re-layouts: 4.82 us -> none  [pick(): return lax.dynamic_index_in_dim(x, index, 0, keepdims=False)]
    reshape x2 -> x1, local copies, waits for them, and re-layouts: 2.65 us -> 0.09 us  [on_device(): groups.reshape(query_len, 1)]
    convert_element_type x5 -> x1, other arithmetic: 2.31 us -> 0.78 us  [on_device(): return (projected, loss, query_grad, cache_part.T.astype(f32))]
  transfers between devices with their start and end apart: 33 -> 27, of which waited for: 21 -> 16; matrix products, arithmetic and copies ran while one was open for 12% -> 2% of each run, Pallas kernels for 0% -> 0%
where the time goes in v2:
time: 91 us; the launch traced here: 90.8 us
  waiting for transfers between devices  37.7 us (41%)
  starting transfers between devices  26.8 us (29%)
  Pallas kernels  15.8 us (17%)
  local copies, waits for them, and re-layouts  4.8 us (5%)
  between operations  2.73 us (3%)
  other arithmetic  1.61 us (2%)
  matrix products  1.25 us (1%)
    ppermute x27, waiting for transfers between devices, swap(): return lax.ppermute(x, axis, [(i, i ^ k * stride) for i in range(n)])  37.7 us
    ppermute x27, starting transfers between devices, swap(): return lax.ppermute(x, axis, [(i, i ^ k * stride) for i in range(n)])  26.8 us
    pallas_call x9, Pallas kernels, call(): pl.pallas_call(kernel, out_shape=out_shape, in_specs=specs or [vmem] * le...  15.8 us
    unnamed x19, local copies, waits for them, and re-layouts  4.6 us
  transfers between devices with their start and end apart: 27, of which 16 were waited for; matrix products, arithmetic and copies ran while one was open for 2% of the time, Pallas kernels for 0%

profile of v2, /device:TPU:0, one launch (start us, length us, event | category | flops | bytes accessed | tf_op | source)
XLA Modules:
  0.0 90.8 jit_solution(914922289693855104)
XLA Ops:
  0.7 1.4 %copy.11.cache_ref = bf16[512,576]{1,0:T(8,128)(2,1)S(1)} copy(bf16[512,576]{0,1:T(8,128)(2,1)} %param.8) | data formatting | bytes 1179648 | tf_op args[1]
  2.1 0.1 copy.12.grp_ref
  2.2 6.1 %shard_map.102 = (bf16[17,24,128]{2,1,0:T(8,128)(2,1)S(1)}, bf16[17,24,128]{2,1,0:T(8,128)(2,1)S(1)}, f32[768,512]{1,0:T(8,128)S(1)}, f32[2,2,24,128]{3,2,1,0:T(8,128)S(1)}, bf16[768,576]{1,0:T(8,128)(2,1)S(1)}) custom-call(bf16[768,576]{1,0:T(8,128)(2,1)S(1)} %bitcast.40, bf16[512,576]{1,0:T(8,128)(2,1)S(1)} %copy.11.cache_ref, s32[1,512]{1,0:T(1,128)S(1)} %bitcast.44, ...), custom_call_target="tpu_custom_call" | custom-call | flops 956301312 | bytes 5671008 | tf_op jit(solution)/shard_map/pallas_call | solution.py:73
  8.3 0.0 copy-start.2
  8.3 0.9 %copy-done.2 = bf16[768,576]{1,0:T(8,128)(2,1)} copy-done((bf16[768,576]{1,0:T(8,128)(2,1)}, bf16[768,576]{1,0:T(8,128)(2,1)S(1)}, u32[]{:S(2)}) %copy-start.2) | copy-done | bytes 884760
  9.2 0.5 collective-permute-start
  9.7 1.0 %collective-permute-done.refs_1_ = bf16[17,24,128]{2,1,0:T(8,128)(2,1)S(1)} collective-permute-done((bf16[17,24,128]{2,1,0:T(8,128)(2,1)S(1)}, bf16[17,24,128]{2,1,0:T(8,128)(2,1)S(1)}, u32[]{:S(2)}, u32[]{:S(2)}) %collective-permute-start) | collective-permute-done | bytes 104480 | tf_op jit(solution)/shard_map/ppermute | solution.py:38
  10.7 0.3 shard_map.103.refs_0_
  11.0 0.0 slice-start.1
  11.1 3.0 %collective-permute-start.1 = (bf16[17,24,128]{2,1,0:T(8,128)(2,1)S(1)}, bf16[17,24,128]{2,1,0:T(8,128)(2,1)S(1)}, u32[]{:S(2)}, u32[]{:S(2)}) collective-permute-start(bf16[17,24,128]{2,1,0:T(8,128)(2,1)S(1)} %shard_map.103.refs_0_), channel_id=1, source_target_pairs={{0,2},{1,3},{2,0},{3,1},{4,6},{5,7},{6,4},{7,5},{8,10},{9,11},{10,... | collective-permute-start | bytes 313352 | tf_op jit(solution)/shard_map/ppermute | solution.py:38
  14.0 2.6 %collective-permute-start.2 = (bf16[17,24,128]{2,1,0:T(8,128)(2,1)S(1)}, bf16[17,24,128]{2,1,0:T(8,128)(2,1)S(1)}, u32[]{:S(2)}, u32[]{:S(2)}) collective-permute-start(bf16[17,24,128]{2,1,0:T(8,128)(2,1)S(1)} %shard_map.103.refs_0_), channel_id=1, source_target_pairs={{0,4},{1,5},{2,6},{3,7},{4,0},{5,1},{6,2},{7,3},{8,12},{9,13},{10,... | collective-permute-start | bytes 313352 | tf_op jit(solution)/shard_map/ppermute | solution.py:38
  16.6 0.0 collective-permute-start.3
  16.6 0.6 collective-permute-done.1.refs_1_
  17.3 7.8 %collective-permute-done.2.refs_2_ = bf16[17,24,128]{2,1,0:T(8,128)(2,1)S(1)} collective-permute-done((bf16[17,24,128]{2,1,0:T(8,128)(2,1)S(1)}, bf16[17,24,128]{2,1,0:T(8,128)(2,1)S(1)}, u32[]{:S(2)}, u32[]{:S(2)}) %collective-permute-start.2) | collective-permute-done | bytes 104480 | tf_op jit(solution)/shard_map/ppermute | solution.py:38
  25.1 0.5 shard_map.104.val_ref
  25.5 0.0 copy-start.4
  25.6 0.1 collective-permute-start.4
  25.6 1.3 %collective-permute-done.4.val_got_ref = bf16[17,24,128]{2,1,0:T(8,128)(2,1)S(1)} collective-permute-done((bf16[17,24,128]{2,1,0:T(8,128)(2,1)S(1)}, bf16[17,24,128]{2,1,0:T(8,128)(2,1)S(1)}, u32[]{:S(2)}, u32[]{:S(2)}) %collective-permute-start.4) | collective-permute-done | bytes 104480 | tf_op jit(solution)/shard_map/ppermute | solution.py:38
  26.9 1.3 %shard_map.105.refs_0_ = bf16[24,896]{1,0:T(8,128)(2,1)S(1)} custom-call(bf16[17,24,128]{2,1,0:T(8,128)(2,1)S(1)} %shard_map.104.val_ref, bf16[17,24,128]{2,1,0:T(8,128)(2,1)S(1)} %collective-permute-done.4.val_got_ref, bf16[4096,896]{1,0:T(8,128)(2,1)S(1)} %bitcast.39), custom_call_target="tpu_custom_call" | custom-call | flops 176160768 | bytes 7548928 | tf_op jit(solution)/shard_map/pallas_call | solution.py:73
  28.2 1.6 %collective-permute-start.5 = (bf16[24,896]{1,0:T(8,128)(2,1)S(1)}, bf16[24,896]{1,0:T(8,128)(2,1)S(1)}, u32[]{:S(2)}, u32[]{:S(2)}) collective-permute-start(bf16[24,896]{1,0:T(8,128)(2,1)S(1)} %shard_map.105.refs_0_), channel_id=1, source_target_pairs={{0,8},{8,0},{16,24},{24,16},{1,9},{9,1},{17,25},{25,17},{2,10},{10... | collective-permute-start | bytes 129032 | tf_op jit(solution)/shard_map/ppermute | solution.py:38
  29.8 1.5 %collective-permute-start.6 = (bf16[24,896]{1,0:T(8,128)(2,1)S(1)}, bf16[24,896]{1,0:T(8,128)(2,1)S(1)}, u32[]{:S(2)}, u32[]{:S(2)}) collective-permute-start(bf16[24,896]{1,0:T(8,128)(2,1)S(1)} %shard_map.105.refs_0_), channel_id=1, source_target_pairs={{0,16},{8,24},{16,0},{24,8},{1,17},{9,25},{17,1},{25,9},{2,18},{10... | collective-permute-start | bytes 129032 | tf_op jit(solution)/shard_map/ppermute | solution.py:38
  31.3 0.5 collective-permute-start.7
  31.8 0.5 collective-permute-done.5.refs_1_
  32.3 1.5 %collective-permute-done.6.refs_2_ = bf16[24,896]{1,0:T(8,128)(2,1)S(1)} collective-permute-done((bf16[24,896]{1,0:T(8,128)(2,1)S(1)}, bf16[24,896]{1,0:T(8,128)(2,1)S(1)}, u32[]{:S(2)}, u32[]{:S(2)}) %collective-permute-start.6) | collective-permute-done | bytes 43040 | tf_op jit(solution)/shard_map/ppermute | solution.py:38
  33.8 2.4 %collective-permute-done.7.refs_3_ = bf16[24,896]{1,0:T(8,128)(2,1)S(1)} collective-permute-done((bf16[24,896]{1,0:T(8,128)(2,1)S(1)}, bf16[24,896]{1,0:T(8,128)(2,1)S(1)}, u32[]{:S(2)}, u32[]{:S(2)}) %collective-permute-start.7) | collective-permute-done | bytes 43040 | tf_op jit(solution)/shard_map/ppermute | solution.py:38
  36.2 2.3 %shard_map.106 = (f32[24,896]{1,0:T(8,128)}, bf16[17,24,128]{2,1,0:T(8,128)(2,1)S(1)}, bf16[17,24,128]{2,1,0:T(8,128)(2,1)S(1)}) custom-call(bf16[24,896]{1,0:T(8,128)(2,1)S(1)} %shard_map.105.refs_0_, bf16[24,896]{1,0:T(8,128)(2,1)S(1)} %collective-permute-done.5.refs_1_, bf16[24,896]{1,0:T(8,128)(2,1)S(1)} %collective-permute-done.6.refs_2_, ...), custom_call_target="tpu_custom_call" | custom-call | flops 176160768 | bytes 7598080 | tf_op jit(solution)/shard_map/pallas_call | solution.py:73
  38.5 0.1 collective-permute-start.8
  38.6 1.3 %collective-permute-done.8.refs_1_ = bf16[17,24,128]{2,1,0:T(8,128)(2,1)S(1)} collective-permute-done((bf16[17,24,128]{2,1,0:T(8,128)(2,1)S(1)}, bf16[17,24,128]{2,1,0:T(8,128)(2,1)S(1)}, u32[]{:S(2)}, u32[]{:S(2)}) %collective-permute-start.8) | collective-permute-done | bytes 104480 | tf_op jit(solution)/shard_map/ppermute | solution.py:38
  40.0 3.0 %collective-permute-start.10 = (bf16[17,24,128]{2,1,0:T(8,128)(2,1)S(1)}, bf16[17,24,128]{2,1,0:T(8,128)(2,1)S(1)}, u32[]{:S(2)}, u32[]{:S(2)}) collective-permute-start(bf16[17,24,128]{2,1,0:T(8,128)(2,1)S(1)} %shard_map.107.refs_0_), channel_id=1, source_target_pairs={{0,4},{1,5},{2,6},{3,7},{4,0},{5,1},{6,2},{7,3},{8,12},{9,13},{10,... | collective-permute-start | bytes 313352 | tf_op jit(solution)/shard_map/ppermute | solution.py:38
  42.9 1.3 %collective-permute-start.11 = (bf16[17,24,128]{2,1,0:T(8,128)(2,1)S(1)}, bf16[17,24,128]{2,1,0:T(8,128)(2,1)S(1)}, u32[]{:S(2)}, u32[]{:S(2)}) collective-permute-start(bf16[17,24,128]{2,1,0:T(8,128)(2,1)S(1)} %shard_map.107.refs_0_), channel_id=1, source_target_pairs={{0,6},{1,7},{2,4},{3,5},{4,2},{5,3},{6,0},{7,1},{8,14},{9,15},{10,... | collective-permute-start | bytes 313352 | tf_op jit(solution)/shard_map/ppermute | solution.py:38
  44.2 7.0 %collective-permute-done.10.refs_2_ = bf16[17,24,128]{2,1,0:T(8,128)(2,1)S(1)} collective-permute-done((bf16[17,24,128]{2,1,0:T(8,128)(2,1)S(1)}, bf16[17,24,128]{2,1,0:T(8,128)(2,1)S(1)}, u32[]{:S(2)}, u32[]{:S(2)}) %collective-permute-start.10) | collective-permute-done | bytes 104480 | tf_op jit(solution)/shard_map/ppermute | solution.py:38
  51.2 0.7 collective-permute-done.9.refs_1_
  52.0 0.1 shard_map.108.dv_ref
  52.1 0.1 collective-permute-start.12
  52.2 1.2 %collective-permute-done.12.dv_got_ref = bf16[17,24,128]{2,1,0:T(8,128)(2,1)S(1)} collective-permute-done((bf16[17,24,128]{2,1,0:T(8,128)(2,1)S(1)}, bf16[17,24,128]{2,1,0:T(8,128)(2,1)S(1)}, u32[]{:S(2)}, u32[]{:S(2)}) %collective-permute-start.12) | collective-permute-done | bytes 104480 | tf_op jit(solution)/shard_map/ppermute | solution.py:38
  53.4 2.2 %copy-done = bf16[32,512,128]{2,1,0:T(8,128)(2,1)S(1)} copy-done((bf16[32,512,128]{2,1,0:T(8,128)(2,1)S(1)}, bf16[32,512,128]{2,1,0:T(8,128)(2,1)}, u32[]{:S(2)}) %copy-start) | copy-done | bytes 4194328
  55.6 3.8 %shard_map.109 = (bf16[2,8,216,128]{3,2,1,0:T(8,128)(2,1)S(1)}, bf16[32,24,512]{2,1,0:T(8,128)(2,1)S(1)}, bf16[32,24,512]{2,1,0:T(8,128)(2,1)S(1)}, bf16[32,24,512]{2,1,0:T(8,128)(2,1)S(1)}) custom-call(bf16[17,24,128]{2,1,0:T(8,128)(2,1)S(1)} %shard_map.108.dv_ref, bf16[17,24,128]{2,1,0:T(8,128)(2,1)S(1)} %collective-permute-done.12.dv_got_ref, ...), custom_call_target="tpu_custom_call" | custom-call | flops 478150656 | bytes 6823936 | tf_op jit(solution)/shard_map/pallas_call | solution.py:73
  59.4 0.7 fusion.8
  60.1 0.2 collective-permute-start.13
  60.3 0.6 fusion
  61.0 1.0 %collective-permute-done.13 = bf16[1728,128]{1,0:T(8,128)(2,1)S(1)} collective-permute-done((bf16[1728,128]{1,0:T(8,128)(2,1)S(1)}, bf16[1728,128]{1,0:T(8,128)(2,1)S(1)}, u32[]{:S(2)}, u32[]{:S(2)}) %collective-permute-start.13) | collective-permute-done | bytes 442400 | tf_op jit(solution)/shard_map/ppermute | solution.py:38
  62.0 0.1 fusion.1
  62.2 2.4 %collective-permute-start.14 = (bf16[432,128]{1,0:T(8,128)(2,1)S(1)}, bf16[432,128]{1,0:T(8,128)(2,1)S(1)}, u32[]{:S(2)}, u32[]{:S(2)}) collective-permute-start(bf16[432,128]{1,0:T(8,128)(2,1)S(1)} %get-tuple-element.31), channel_id=1, source_target_pairs={{0,6},{1,7},{2,4},{3,5},{4,2},{5,3},{6,0},{7,1},{8,14},{9,15},{10,... | collective-permute-start | bytes 331784 | tf_op jit(solution)/shard_map/ppermute | solution.py:38
  64.6 0.6 collective-permute-start.15
  65.2 1.4 %collective-permute-start.16 = (bf16[432,128]{1,0:T(8,128)(2,1)S(1)}, bf16[432,128]{1,0:T(8,128)(2,1)S(1)}, u32[]{:S(2)}, u32[]{:S(2)}) collective-permute-start(bf16[432,128]{1,0:T(8,128)(2,1)S(1)} %get-tuple-element.32), channel_id=1, source_target_pairs={{0,2},{1,3},{2,0},{3,1},{4,6},{5,7},{6,4},{7,5},{8,10},{9,11},{10,... | collective-permute-start | bytes 331784 | tf_op jit(solution)/shard_map/ppermute | solution.py:38
  66.6 0.5 collective-permute-start.24
  67.2 1.5 %collective-permute-start.25 = (bf16[144,512]{1,0:T(8,128)(2,1)S(1)}, bf16[144,512]{1,0:T(8,128)(2,1)S(1)}, u32[]{:S(2)}, u32[]{:S(2)}) collective-permute-start(bf16[144,512]{1,0:T(8,128)(2,1)S(1)} %get-tuple-element.30), channel_id=1, source_target_pairs={{0,16},{8,24},{16,0},{24,8},{1,17},{9,25},{17,1},{25,9},{2,18},{10... | collective-permute-start | bytes 442376 | tf_op jit(solution)/shard_map/ppermute | solution.py:38
  68.7 1.4 %collective-permute-done.14 = bf16[432,128]{1,0:T(8,128)(2,1)S(1)} collective-permute-done((bf16[432,128]{1,0:T(8,128)(2,1)S(1)}, bf16[432,128]{1,0:T(8,128)(2,1)S(1)}, u32[]{:S(2)}, u32[]{:S(2)}) %collective-permute-start.14) | collective-permute-done | bytes 110624 | tf_op jit(solution)/shard_map/ppermute | solution.py:38
  70.1 0.5 collective-permute-start.26
  70.6 4.8 %collective-permute-done.15 = bf16[432,128]{1,0:T(8,128)(2,1)S(1)} collective-permute-done((bf16[432,128]{1,0:T(8,128)(2,1)S(1)}, bf16[432,128]{1,0:T(8,128)(2,1)S(1)}, u32[]{:S(2)}, u32[]{:S(2)}) %collective-permute-start.15) | collective-permute-done | bytes 110624 | tf_op jit(solution)/shard_map/ppermute | solution.py:38
  75.4 0.1 fusion.7.refs_0_
  75.4 0.1 collective-permute-start.17
  75.5 2.9 %collective-permute-start.18 = (bf16[432,128]{1,0:T(8,128)(2,1)S(1)}, bf16[432,128]{1,0:T(8,128)(2,1)S(1)}, u32[]{:S(2)}, u32[]{:S(2)}) collective-permute-start(bf16[432,128]{1,0:T(8,128)(2,1)S(1)} %fusion.7.refs_0_), channel_id=1, source_target_pairs={{0,4},{1,5},{2,6},{3,7},{4,0},{5,1},{6,2},{7,3},{8,12},{9,13},{10,... | collective-permute-start | bytes 331784 | tf_op jit(solution)/shard_map/ppermute | solution.py:38
  78.4 1.5 %collective-permute-start.19 = (bf16[432,128]{1,0:T(8,128)(2,1)S(1)}, bf16[432,128]{1,0:T(8,128)(2,1)S(1)}, u32[]{:S(2)}, u32[]{:S(2)}) collective-permute-start(bf16[432,128]{1,0:T(8,128)(2,1)S(1)} %fusion.7.refs_0_), channel_id=1, source_target_pairs={{0,6},{1,7},{2,4},{3,5},{4,2},{5,3},{6,0},{7,1},{8,14},{9,15},{10,... | collective-permute-start | bytes 331784 | tf_op jit(solution)/shard_map/ppermute | solution.py:38
  79.9 0.6 convert_reduce_fusion
  81.2 0.1 collective-permute-start.20
  81.2 0.0 collective-permute-done.17.refs_1_
  81.3 0.5 collective-permute-start.21
  81.7 5.0 %collective-permute-done.18.refs_2_ = bf16[432,128]{1,0:T(8,128)(2,1)S(1)} collective-permute-done((bf16[432,128]{1,0:T(8,128)(2,1)S(1)}, bf16[432,128]{1,0:T(8,128)(2,1)S(1)}, u32[]{:S(2)}, u32[]{:S(2)}) %collective-permute-start.18) | collective-permute-done | bytes 110624 | tf_op jit(solution)/shard_map/ppermute | solution.py:38
  86.7 0.5 collective-permute-start.23
  87.2 0.8 convert_bitcast_fusion
  88.0 0.0 collective-permute-done.22.refs_6_
  88.0 0.2 collective-permute-done.23.refs_7_
  88.2 1.5 %shard_map.110 = f32[24,32,576]{2,1,0:T(8,128)} custom-call(bf16[432,128]{1,0:T(8,128)(2,1)S(1)} %fusion.7.refs_0_, bf16[432,128]{1,0:T(8,128)(2,1)S(1)} %collective-permute-done.17.refs_1_, bf16[432,128]{1,0:T(8,128)(2,1)S(1)} %collective-permute-done.18.refs_2_, bf16[432,128]{1,0:T(8,128)(2,1)S(1)} %collective-permute-done.19.refs_3_, ...), custom_call_target="tpu_custom_call" | custom-call | bytes 884736 | tf_op jit(solution)/shard_map/pallas_call | solution.py:73
  (31 shorter events, 0.3 us)
Async XLA Ops:
  0.6 1.5 %copy-start.6 = (s32[24]{0:T(128)S(1)}, s32[24]{0:T(128)}, u32[]{:S(2)}) copy-start(s32[24]{0:T(128)} %param.10) | copy-start | bytes 292
  0.6 1.6 %copy-start.1 = (bf16[24,32,576]{2,1,0:T(8,128)(2,1)S(1)}, bf16[24,32,576]{2,1,0:T(8,128)(2,1)}, u32[]{:S(2)}) copy-start(bf16[24,32,576]{2,1,0:T(8,128)(2,1)} %param.7) | copy-start | bytes 2654212
  0.7 1.6 %copy-start.5 = (s32[512]{0:T(512)S(1)}, s32[512]{0:T(512)}, u32[]{:S(2)}) copy-start(s32[512]{0:T(512)} %param.9) | copy-start | bytes 6148
  2.2 24.7 %slice-start = ((s8[7340032]{0:T(1024)(128)(4,1)}), s8[3145728]{0:T(1024)(128)(4,1)S(1)}, s32[]{:S(2)}) async-start(s8[7340032]{0:T(1024)(128)(4,1)} %bitcast.38), calls=%async_computation | async-start | bytes 6291456
  8.3 0.9 %copy-start.2 = (bf16[768,576]{1,0:T(8,128)(2,1)}, bf16[768,576]{1,0:T(8,128)(2,1)S(1)}, u32[]{:S(2)}) copy-start(bf16[768,576]{1,0:T(8,128)(2,1)S(1)} %get-tuple-element.24) | copy-start | bytes 2654212
  9.2 1.5 %collective-permute-start = (bf16[17,24,128]{2,1,0:T(8,128)(2,1)S(1)}, bf16[17,24,128]{2,1,0:T(8,128)(2,1)S(1)}, u32[]{:S(2)}, u32[]{:S(2)}) collective-permute-start(bf16[17,24,128]{2,1,0:T(8,128)(2,1)S(1)} %get-tuple-element.17), channel_id=1, source_target_pairs={{0,1},{1,0},{2,3},{3,2},{4,5},{5,4},{6,7},{7,6},{8,9},{9,8},{10,11... | collective-permute-start | bytes 313352 | tf_op jit(solution)/shard_map/ppermute | solution.py:38
  11.0 15.9 %slice-start.1 = ((s8[7340032]{0:T(1024)(128)(4,1)}), s8[4194304]{0:T(1024)(128)(4,1)S(1)}, s32[]{:S(2)}) async-start(s8[7340032]{0:T(1024)(128)(4,1)} %bitcast.38), calls=%async_computation.1 | async-start | bytes 8388608
  11.1 6.2 %collective-permute-start.1 = (bf16[17,24,128]{2,1,0:T(8,128)(2,1)S(1)}, bf16[17,24,128]{2,1,0:T(8,128)(2,1)S(1)}, u32[]{:S(2)}, u32[]{:S(2)}) collective-permute-start(bf16[17,24,128]{2,1,0:T(8,128)(2,1)S(1)} %shard_map.103.refs_0_), channel_id=1, source_target_pairs={{0,2},{1,3},{2,0},{3,1},{4,6},{5,7},{6,4},{7,5},{8,10},{9,11},{10,... | collective-permute-start | bytes 313352 | tf_op jit(solution)/shard_map/ppermute | solution.py:38
  14.0 11.0 %collective-permute-start.2 = (bf16[17,24,128]{2,1,0:T(8,128)(2,1)S(1)}, bf16[17,24,128]{2,1,0:T(8,128)(2,1)S(1)}, u32[]{:S(2)}, u32[]{:S(2)}) collective-permute-start(bf16[17,24,128]{2,1,0:T(8,128)(2,1)S(1)} %shard_map.103.refs_0_), channel_id=1, source_target_pairs={{0,4},{1,5},{2,6},{3,7},{4,0},{5,1},{6,2},{7,3},{8,12},{9,13},{10,... | collective-permute-start | bytes 313352 | tf_op jit(solution)/shard_map/ppermute | solution.py:38
  16.6 8.4 %collective-permute-start.3 = (bf16[17,24,128]{2,1,0:T(8,128)(2,1)S(1)}, bf16[17,24,128]{2,1,0:T(8,128)(2,1)S(1)}, u32[]{:S(2)}, u32[]{:S(2)}) collective-permute-start(bf16[17,24,128]{2,1,0:T(8,128)(2,1)S(1)} %shard_map.103.refs_0_), channel_id=1, source_target_pairs={{0,6},{1,7},{2,4},{3,5},{4,2},{5,3},{6,0},{7,1},{8,14},{9,15},{10,... | collective-permute-start | bytes 313352 | tf_op jit(solution)/shard_map/ppermute | solution.py:38
  25.5 10.7 %copy-start.4 = (f32[24,896]{1,0:T(8,128)S(1)}, f32[24,896]{1,0:T(8,128)}, u32[]{:S(2)}) copy-start(f32[24,896]{1,0:T(8,128)} %refs_4_.1) | copy-start | bytes 258052
  25.6 1.4 %collective-permute-start.4 = (bf16[17,24,128]{2,1,0:T(8,128)(2,1)S(1)}, bf16[17,24,128]{2,1,0:T(8,128)(2,1)S(1)}, u32[]{:S(2)}, u32[]{:S(2)}) collective-permute-start(bf16[17,24,128]{2,1,0:T(8,128)(2,1)S(1)} %shard_map.104.val_ref), channel_id=1, source_target_pairs={{0,1},{1,0},{2,3},{3,2},{4,5},{5,4},{6,7},{7,6},{8,9},{9,8},{10,11... | collective-permute-start | bytes 313352 | tf_op jit(solution)/shard_map/ppermute | solution.py:38
  28.2 4.1 %collective-permute-start.5 = (bf16[24,896]{1,0:T(8,128)(2,1)S(1)}, bf16[24,896]{1,0:T(8,128)(2,1)S(1)}, u32[]{:S(2)}, u32[]{:S(2)}) collective-permute-start(bf16[24,896]{1,0:T(8,128)(2,1)S(1)} %shard_map.105.refs_0_), channel_id=1, source_target_pairs={{0,8},{8,0},{16,24},{24,16},{1,9},{9,1},{17,25},{25,17},{2,10},{10... | collective-permute-start | bytes 129032 | tf_op jit(solution)/shard_map/ppermute | solution.py:38
  29.8 4.0 %collective-permute-start.6 = (bf16[24,896]{1,0:T(8,128)(2,1)S(1)}, bf16[24,896]{1,0:T(8,128)(2,1)S(1)}, u32[]{:S(2)}, u32[]{:S(2)}) collective-permute-start(bf16[24,896]{1,0:T(8,128)(2,1)S(1)} %shard_map.105.refs_0_), channel_id=1, source_target_pairs={{0,16},{8,24},{16,0},{24,8},{1,17},{9,25},{17,1},{25,9},{2,18},{10... | collective-permute-start | bytes 129032 | tf_op jit(solution)/shard_map/ppermute | solution.py:38
  31.3 4.9 %collective-permute-start.7 = (bf16[24,896]{1,0:T(8,128)(2,1)S(1)}, bf16[24,896]{1,0:T(8,128)(2,1)S(1)}, u32[]{:S(2)}, u32[]{:S(2)}) collective-permute-start(bf16[24,896]{1,0:T(8,128)(2,1)S(1)} %shard_map.105.refs_0_), channel_id=1, source_target_pairs={{0,24},{8,16},{16,8},{24,0},{1,25},{9,17},{17,9},{25,1},{2,26},{10... | collective-permute-start | bytes 129032 | tf_op jit(solution)/shard_map/ppermute | solution.py:38
  38.5 1.4 %collective-permute-start.8 = (bf16[17,24,128]{2,1,0:T(8,128)(2,1)S(1)}, bf16[17,24,128]{2,1,0:T(8,128)(2,1)S(1)}, u32[]{:S(2)}, u32[]{:S(2)}) collective-permute-start(bf16[17,24,128]{2,1,0:T(8,128)(2,1)S(1)} %get-tuple-element.20), channel_id=1, source_target_pairs={{0,1},{1,0},{2,3},{3,2},{4,5},{5,4},{6,7},{7,6},{8,9},{9,8},{10,11... | collective-permute-start | bytes 313352 | tf_op jit(solution)/shard_map/ppermute | solution.py:38
  40.0 11.3 %collective-permute-start.10 = (bf16[17,24,128]{2,1,0:T(8,128)(2,1)S(1)}, bf16[17,24,128]{2,1,0:T(8,128)(2,1)S(1)}, u32[]{:S(2)}, u32[]{:S(2)}) collective-permute-start(bf16[17,24,128]{2,1,0:T(8,128)(2,1)S(1)} %shard_map.107.refs_0_), channel_id=1, source_target_pairs={{0,4},{1,5},{2,6},{3,7},{4,0},{5,1},{6,2},{7,3},{8,12},{9,13},{10,... | collective-permute-start | bytes 313352 | tf_op jit(solution)/shard_map/ppermute | solution.py:38
  42.9 8.3 %collective-permute-start.11 = (bf16[17,24,128]{2,1,0:T(8,128)(2,1)S(1)}, bf16[17,24,128]{2,1,0:T(8,128)(2,1)S(1)}, u32[]{:S(2)}, u32[]{:S(2)}) collective-permute-start(bf16[17,24,128]{2,1,0:T(8,128)(2,1)S(1)} %shard_map.107.refs_0_), channel_id=1, source_target_pairs={{0,6},{1,7},{2,4},{3,5},{4,2},{5,3},{6,0},{7,1},{8,14},{9,15},{10,... | collective-permute-start | bytes 313352 | tf_op jit(solution)/shard_map/ppermute | solution.py:38
  44.2 7.8 %collective-permute-start.9 = (bf16[17,24,128]{2,1,0:T(8,128)(2,1)S(1)}, bf16[17,24,128]{2,1,0:T(8,128)(2,1)S(1)}, u32[]{:S(2)}, u32[]{:S(2)}) collective-permute-start(bf16[17,24,128]{2,1,0:T(8,128)(2,1)S(1)} %shard_map.107.refs_0_), channel_id=1, source_target_pairs={{0,2},{1,3},{2,0},{3,1},{4,6},{5,7},{6,4},{7,5},{8,10},{9,11},{10,... | collective-permute-start | bytes 313352 | tf_op jit(solution)/shard_map/ppermute | solution.py:38
  52.1 1.4 %collective-permute-start.12 = (bf16[17,24,128]{2,1,0:T(8,128)(2,1)S(1)}, bf16[17,24,128]{2,1,0:T(8,128)(2,1)S(1)}, u32[]{:S(2)}, u32[]{:S(2)}) collective-permute-start(bf16[17,24,128]{2,1,0:T(8,128)(2,1)S(1)} %shard_map.108.dv_ref), channel_id=1, source_target_pairs={{0,1},{1,0},{2,3},{3,2},{4,5},{5,4},{6,7},{7,6},{8,9},{9,8},{10,11... | collective-permute-start | bytes 313352 | tf_op jit(solution)/shard_map/ppermute | solution.py:38
  53.4 2.2 %copy-start = (bf16[32,512,128]{2,1,0:T(8,128)(2,1)S(1)}, bf16[32,512,128]{2,1,0:T(8,128)(2,1)}, u32[]{:S(2)}) copy-start(bf16[32,512,128]{2,1,0:T(8,128)(2,1)} %up_ref.1) | copy-start | bytes 12582916
  55.6 3.8 %copy-start.3 = (bf16[768,576]{1,0:T(8,128)(2,1)S(1)}, bf16[768,576]{1,0:T(8,128)(2,1)}, u32[]{:S(2)}) copy-start(bf16[768,576]{1,0:T(8,128)(2,1)} %copy-done.2) | copy-start | bytes 2654212
  60.1 1.9 %collective-permute-start.13 = (bf16[1728,128]{1,0:T(8,128)(2,1)S(1)}, bf16[1728,128]{1,0:T(8,128)(2,1)S(1)}, u32[]{:S(2)}, u32[]{:S(2)}) collective-permute-start(bf16[1728,128]{1,0:T(8,128)(2,1)S(1)} %dynamic-slice_bitcast_fusion), channel_id=1, source_target_pairs={{0,1},{1,0},{2,3},{3,2},{4,5},{5,4},{6,7},{7,6},{8,9},{9,8},{10,11... | collective-permute-start | bytes 1327112 | tf_op jit(solution)/shard_map/ppermute | solution.py:38
  62.2 7.9 %collective-permute-start.14 = (bf16[432,128]{1,0:T(8,128)(2,1)S(1)}, bf16[432,128]{1,0:T(8,128)(2,1)S(1)}, u32[]{:S(2)}, u32[]{:S(2)}) collective-permute-start(bf16[432,128]{1,0:T(8,128)(2,1)S(1)} %get-tuple-element.31), channel_id=1, source_target_pairs={{0,6},{1,7},{2,4},{3,5},{4,2},{5,3},{6,0},{7,1},{8,14},{9,15},{10,... | collective-permute-start | bytes 331784 | tf_op jit(solution)/shard_map/ppermute | solution.py:38
  64.6 10.8 %collective-permute-start.15 = (bf16[432,128]{1,0:T(8,128)(2,1)S(1)}, bf16[432,128]{1,0:T(8,128)(2,1)S(1)}, u32[]{:S(2)}, u32[]{:S(2)}) collective-permute-start(bf16[432,128]{1,0:T(8,128)(2,1)S(1)} %get-tuple-element.33), channel_id=1, source_target_pairs={{0,4},{1,5},{2,6},{3,7},{4,0},{5,1},{6,2},{7,3},{8,12},{9,13},{10,... | collective-permute-start | bytes 331784 | tf_op jit(solution)/shard_map/ppermute | solution.py:38
  65.2 10.2 %collective-permute-start.16 = (bf16[432,128]{1,0:T(8,128)(2,1)S(1)}, bf16[432,128]{1,0:T(8,128)(2,1)S(1)}, u32[]{:S(2)}, u32[]{:S(2)}) collective-permute-start(bf16[432,128]{1,0:T(8,128)(2,1)S(1)} %get-tuple-element.32), channel_id=1, source_target_pairs={{0,2},{1,3},{2,0},{3,1},{4,6},{5,7},{6,4},{7,5},{8,10},{9,11},{10,... | collective-permute-start | bytes 331784 | tf_op jit(solution)/shard_map/ppermute | solution.py:38
  66.6 11.7 %collective-permute-start.24 = (bf16[144,512]{1,0:T(8,128)(2,1)S(1)}, bf16[144,512]{1,0:T(8,128)(2,1)S(1)}, u32[]{:S(2)}, u32[]{:S(2)}) collective-permute-start(bf16[144,512]{1,0:T(8,128)(2,1)S(1)} %get-tuple-element.28), channel_id=1, source_target_pairs={{0,24},{8,16},{16,8},{24,0},{1,25},{9,17},{17,9},{25,1},{2,26},{10... | collective-permute-start | bytes 442376 | tf_op jit(solution)/shard_map/ppermute | solution.py:38
  67.2 14.0 %collective-permute-start.25 = (bf16[144,512]{1,0:T(8,128)(2,1)S(1)}, bf16[144,512]{1,0:T(8,128)(2,1)S(1)}, u32[]{:S(2)}, u32[]{:S(2)}) collective-permute-start(bf16[144,512]{1,0:T(8,128)(2,1)S(1)} %get-tuple-element.30), channel_id=1, source_target_pairs={{0,16},{8,24},{16,0},{24,8},{1,17},{9,25},{17,1},{25,9},{2,18},{10... | collective-permute-start | bytes 442376 | tf_op jit(solution)/shard_map/ppermute | solution.py:38
  70.1 17.2 %collective-permute-start.26 = (bf16[144,512]{1,0:T(8,128)(2,1)S(1)}, bf16[144,512]{1,0:T(8,128)(2,1)S(1)}, u32[]{:S(2)}, u32[]{:S(2)}) collective-permute-start(bf16[144,512]{1,0:T(8,128)(2,1)S(1)} %get-tuple-element.29), channel_id=1, source_target_pairs={{0,8},{8,0},{16,24},{24,16},{1,9},{9,1},{17,25},{25,17},{2,10},{10... | collective-permute-start | bytes 442376 | tf_op jit(solution)/shard_map/ppermute | solution.py:38
  75.4 5.8 %collective-permute-start.17 = (bf16[432,128]{1,0:T(8,128)(2,1)S(1)}, bf16[432,128]{1,0:T(8,128)(2,1)S(1)}, u32[]{:S(2)}, u32[]{:S(2)}) collective-permute-start(bf16[432,128]{1,0:T(8,128)(2,1)S(1)} %fusion.7.refs_0_), channel_id=1, source_target_pairs={{0,2},{1,3},{2,0},{3,1},{4,6},{5,7},{6,4},{7,5},{8,10},{9,11},{10,... | collective-permute-start | bytes 331784 | tf_op jit(solution)/shard_map/ppermute | solution.py:38
  75.5 11.2 %collective-permute-start.18 = (bf16[432,128]{1,0:T(8,128)(2,1)S(1)}, bf16[432,128]{1,0:T(8,128)(2,1)S(1)}, u32[]{:S(2)}, u32[]{:S(2)}) collective-permute-start(bf16[432,128]{1,0:T(8,128)(2,1)S(1)} %fusion.7.refs_0_), channel_id=1, source_target_pairs={{0,4},{1,5},{2,6},{3,7},{4,0},{5,1},{6,2},{7,3},{8,12},{9,13},{10,... | collective-permute-start | bytes 331784 | tf_op jit(solution)/shard_map/ppermute | solution.py:38
  78.4 8.3 %collective-permute-start.19 = (bf16[432,128]{1,0:T(8,128)(2,1)S(1)}, bf16[432,128]{1,0:T(8,128)(2,1)S(1)}, u32[]{:S(2)}, u32[]{:S(2)}) collective-permute-start(bf16[432,128]{1,0:T(8,128)(2,1)S(1)} %fusion.7.refs_0_), channel_id=1, source_target_pairs={{0,6},{1,7},{2,4},{3,5},{4,2},{5,3},{6,0},{7,1},{8,14},{9,15},{10,... | collective-permute-start | bytes 331784 | tf_op jit(solution)/shard_map/ppermute | solution.py:38
  81.2 6.9 %collective-permute-start.20 = (bf16[432,128]{1,0:T(8,128)(2,1)S(1)}, bf16[432,128]{1,0:T(8,128)(2,1)S(1)}, u32[]{:S(2)}, u32[]{:S(2)}) collective-permute-start(bf16[432,128]{1,0:T(8,128)(2,1)S(1)} %fusion.7.refs_0_), channel_id=1, source_target_pairs={{0,1},{1,0},{2,3},{3,2},{4,5},{5,4},{6,7},{7,6},{8,9},{9,8},{10,11... | collective-permute-start | bytes 331784 | tf_op jit(solution)/shard_map/ppermute | solution.py:38
  81.3 6.8 %collective-permute-start.21 = (bf16[432,128]{1,0:T(8,128)(2,1)S(1)}, bf16[432,128]{1,0:T(8,128)(2,1)S(1)}, u32[]{:S(2)}, u32[]{:S(2)}) collective-permute-start(bf16[432,128]{1,0:T(8,128)(2,1)S(1)} %collective-permute-done.17.refs_1_), channel_id=1, source_target_pairs={{0,1},{1,0},{2,3},{3,2},{4,5},{5,4},{6,7},{7,6},{8,9},{9,8},{10,11... | collective-permute-start | bytes 331784 | tf_op jit(solution)/shard_map/ppermute | solution.py:38
  86.7 1.3 %collective-permute-start.22 = (bf16[432,128]{1,0:T(8,128)(2,1)S(1)}, bf16[432,128]{1,0:T(8,128)(2,1)S(1)}, u32[]{:S(2)}, u32[]{:S(2)}) collective-permute-start(bf16[432,128]{1,0:T(8,128)(2,1)S(1)} %collective-permute-done.18.refs_2_), channel_id=1, source_target_pairs={{0,1},{1,0},{2,3},{3,2},{4,5},{5,4},{6,7},{7,6},{8,9},{9,8},{10,11... | collective-permute-start | bytes 331784 | tf_op jit(solution)/shard_map/ppermute | solution.py:38
  86.7 1.5 %collective-permute-start.23 = (bf16[432,128]{1,0:T(8,128)(2,1)S(1)}, bf16[432,128]{1,0:T(8,128)(2,1)S(1)}, u32[]{:S(2)}, u32[]{:S(2)}) collective-permute-start(bf16[432,128]{1,0:T(8,128)(2,1)S(1)} %collective-permute-done.19.refs_3_), channel_id=1, source_target_pairs={{0,1},{1,0},{2,3},{3,2},{4,5},{5,4},{6,7},{7,6},{8,9},{9,8},{10,11... | collective-permute-start | bytes 331784 | tf_op jit(solution)/shard_map/ppermute | solution.py:38
